TPU v7x, 32 devices: a whole 2x2x4 slice. The times are simulated.
32 devices in a mesh: wide: 8 (over z, x), narrow: 4 (over y, core).
Axes of the slice: x: 2, y: 2, z: 4, core: 2. Of those that a mesh axis runs over, the one named last changes fastest.
Arguments:
- tokens: bfloat16 [64, 256, 512], P(('wide', 'narrow')), may hold values from -6 to 6
- cotangent: bfloat16 [64, 256, 512], P(('wide', 'narrow')), may hold values from -0.29882812 to 0.29882812
- lengths: int32 [64], P(('wide', 'narrow')), may hold values from 160 to 256, as said below
- item_rows: int32 [64, 256], P(('wide', 'narrow')), may hold values from 0 to 1023, as said below
- w_in: bfloat16 [512, 2048], replicated, may hold values from -0.25 to 0.25
- w_out: bfloat16 [512, 512], replicated, may hold values from -0.25 to 0.25
- table: float32 [1024, 512], P(('wide', 'narrow')), may hold values from -6 to 6
- moment_one: float32 [1024, 512], P(('wide', 'narrow')), may hold values from -0.3 to 0.3
- moment_two: float32 [1024, 512], P(('wide', 'narrow')), may hold values from 0.0001 to 0.01
Outputs:
- table_new: float32 [1024, 512], P(('wide', 'narrow'))
- moment_one_new: float32 [1024, 512], P(('wide', 'narrow'))
- moment_two_new: float32 [1024, 512], P(('wide', 'narrow'))
Inputs may be any that keep to these rules, and one draw needn't show every extreme that they name: `lengths`: some sequence has exactly 256 live positions. `item_rows`: A row r has inner block index (r // 32) % 4. In every sequence at most 128 of the 256 positions name rows of one inner block index, and some index is named by exactly 128 of them.
All inputs are finite; a program needn't handle non-finite values.
Results may differ from a plain program's by a relative error of at most 0.005.
Values may be sent and summed in bfloat16 or wider, within the bound.
No kernel may reach another device: no remote copies, remote signals or barrier semaphores. Data moves between devices by JAX's collectives and lax.ppermute only.
A program may use at most 64 MiB of HBM per device.

v0:
```python
import jax
import jax.numpy as jnp
from jax import lax
from jax.sharding import PartitionSpec as P

HEADS = 8


norm_eps = 1e-06
clip_norm = 4.0
learn_rate = 0.5
beta_first = 0.9
beta_second = 0.999
adam_step = 3.0
adam_eps = 1e-08


def layer_forward(source, w_in, w_out, length):
    positions, width = source.shape
    per_head = width // HEADS
    inner = jnp.dot(source.astype(jnp.bfloat16), w_in, preferred_element_type=jnp.float32)
    hidden = jax.nn.silu(inner).astype(jnp.bfloat16)
    gate_part, value_part, query_part, key_part = jnp.split(hidden, 4, axis=1)
    query_part = query_part.reshape(positions, HEADS, per_head)
    key_part = key_part.reshape(positions, HEADS, per_head)
    value_part = value_part.reshape(positions, HEADS, per_head)
    scores = jnp.einsum(
        "qhd,khd->hqk", query_part, key_part, preferred_element_type=jnp.float32
    ) * per_head ** (-0.5)
    index_row = jnp.arange(positions)
    allowed = ((index_row[None, :] <= index_row[:, None]) & (index_row[:, None] < length)).astype(
        jnp.float32
    )
    attention = (jax.nn.silu(scores) * allowed[None] / length.astype(jnp.float32)).astype(
        jnp.bfloat16
    )
    mixed = jnp.einsum(
        "hqk,khd->qhd", attention, value_part, preferred_element_type=jnp.float32
    ).reshape(positions, width)
    centered = mixed - jnp.mean(mixed, axis=1, keepdims=True)
    normed = centered * lax.rsqrt(jnp.mean(centered * centered, axis=1, keepdims=True) + norm_eps)
    gated = (normed * gate_part.astype(jnp.float32)).astype(jnp.bfloat16)
    return jnp.dot(gated, w_out, preferred_element_type=jnp.float32) + source


def token_grads(inputs, cotangent, length, w_in, w_out):
    live_mask = (jnp.arange(inputs.shape[0]) < length).astype(jnp.float32)
    _, pullback = jax.vjp(
        lambda source_rows: layer_forward(source_rows, w_in, w_out, length),
        inputs.astype(jnp.float32),
    )
    (gradient,) = pullback(cotangent.astype(jnp.float32) * live_mask[:, None])
    return gradient.astype(jnp.bfloat16)


def pack_rows(gradients, row_ids, owners, rows_dev, owned):
    batch_count, slots, width = gradients.shape
    capacity = 2 * slots // owners
    blocks = row_ids // rows_dev
    owner_index = blocks % owners
    local_rows = blocks // owners * rows_dev + row_ids % rows_dev
    hits_table = (owner_index[:, :, None] == jnp.arange(owners)[None, None, :]).astype(jnp.int32)
    ranking = jnp.sum((jnp.cumsum(hits_table, axis=1) - 1) * hits_table, axis=2)
    placed = (
        owner_index * (batch_count * capacity)
        + jnp.arange(batch_count)[:, None] * capacity
        + ranking
    )
    total_slots = owners * batch_count * capacity
    outgoing = (
        jnp.zeros((total_slots, width), jnp.bfloat16)
        .at[placed.reshape(-1)]
        .set(gradients.reshape(-1, width))
    )
    labels = (
        jnp.full((total_slots,), owned, jnp.int32)
        .at[placed.reshape(-1)]
        .set(local_rows.reshape(-1))
    )
    return (
        outgoing.reshape(owners, batch_count * capacity, width),
        labels.reshape(owners, batch_count * capacity),
    )


def owner_total(arrived, arrived_labels, owned):
    row_data = arrived.reshape(-1, arrived.shape[-1])
    flat_labels = arrived_labels.reshape(-1)
    empty = jnp.zeros((owned, row_data.shape[1]), jnp.float32)
    return empty.at[flat_labels].add(row_data.astype(jnp.float32), mode="drop")


def adam_rows(row_grad, table, moment_one, moment_two):
    row_norms = jnp.sqrt(jnp.sum(row_grad * row_grad, axis=1, keepdims=True))
    clipped = row_grad * (clip_norm / jnp.maximum(row_norms, clip_norm))
    first_moment = beta_first * moment_one + (1.0 - beta_first) * clipped
    second_moment = beta_second * moment_two + (1.0 - beta_second) * clipped * clipped
    step_size = learn_rate / (1.0 - beta_first**adam_step)
    scaled = jnp.sqrt(second_moment / (1.0 - beta_second**adam_step)) + adam_eps
    return (table - step_size * first_moment / scaled, first_moment, second_moment)


def on_device(tokens, cotangent, lengths, item_rows, w_in, w_out, table, moment_one, moment_two):
    owners = lax.axis_size("narrow")
    rows_dev = table.shape[0]
    owned = lax.axis_size("wide") * rows_dev
    backward = jax.vmap(token_grads, in_axes=(0, 0, 0, None, None))
    gradients = backward(tokens, cotangent, lengths, w_in, w_out)
    outgoing, labels = pack_rows(gradients, item_rows, owners, rows_dev, owned)
    arrived, arrived_labels = (
        lax.all_to_all(outgoing, "narrow", split_axis=0, concat_axis=0, tiled=True),
        lax.all_to_all(labels, "narrow", split_axis=0, concat_axis=0, tiled=True),
    )
    row_grad = owner_total(arrived, arrived_labels, owned)
    owned_rows = lax.psum_scatter(
        row_grad.astype(jnp.bfloat16), "wide", scatter_dimension=0, tiled=True
    ).astype(jnp.float32)
    return adam_rows(owned_rows, table, moment_one, moment_two)


def solution(mesh):
    return jax.shard_map(
        on_device,
        mesh=mesh,
        in_specs=(
            P(("wide", "narrow"), None, None),
            P(("wide", "narrow"), None, None),
            P(("wide", "narrow")),
            P(("wide", "narrow"), None),
            P(),
            P(),
            P(("wide", "narrow"), None),
            P(("wide", "narrow"), None),
            P(("wide", "narrow"), None),
        ),
        out_specs=(
            P(("wide", "narrow"), None),
            P(("wide", "narrow"), None),
            P(("wide", "narrow"), None),
        ),
        check_vma=False,
    )
```

profile of v0, /device:TPU:0, one launch (start us, length us, event | category | flops | bytes accessed | tf_op | source)
XLA Modules:
  0.0 164.5 jit_solution(587725649173246546)
XLA Ops:
  7.2 0.0 copy-start
  7.2 0.8 fusion.58
  8.1 2.4 %reduce-window.6 = s32[2,4,2,128]{3,2,1,0:T(2,128)S(1)} reduce-window(s32[2,4,2,128]{3,2,1,0:T(2,128)S(1)} %compare_convert_fusion, s32[]{:T(128)} %constant.81.clone.1), window={size=1x1x1x128 pad=0_0x0_0x0_0x127_0}, to_apply=%region_0.1 | reduce-window | flops 260096 | bytes 16388 | tf_op jit(solution)/shard_map/reduce-window
  10.5 0.1 slice.8
  10.6 0.1 copy.25
  10.7 0.1 copy.26
  10.9 0.1 add_add_fusion.1
  11.0 0.1 add_bitcast_fusion
  11.1 3.0 %scatter_custom_fusion = s32[1024]{0:T(1024)} fusion(s32[512]{0:T(512)S(1)} %bitcast.95, s32[512]{0:T(512)S(1)} %bitcast.97, s32[]{:T(128)} %constant.79.clone.1), kind=kCustom, calls=%fused_computation.88 | custom fusion | bytes 4100 | tf_op jit(solution)/shard_map/scatter | solution.py:78
  14.1 4.3 %all-to-all-start = ((s32[4,1,256]{2,1,0:T(1,128)}), s32[4,1,256]{2,1,0:T(1,128)S(1)}, u32[]{:S(2)}, u32[]{:S(2)}) async-start(s32[4,1,256]{2,1,0:T(1,128)} %bitcast.3), calls=%async_computation | async-start | bytes 8192 | tf_op jit(solution)/shard_map/all_to_all | solution.py:112
  18.4 0.7 fusion.62
  19.1 0.7 convert_element_type.98
  19.8 0.0 copy-done
  19.8 4.6 %multiply_convert_fusion = (bf16[2,256,2048]{2,1,0:T(8,128)(2,1)S(1)}, f32[2,256,2048]{2,1,0:T(8,128)}) fusion(bf16[2,256,512]{2,1,0:T(8,128)(2,1)} %param.9, bf16[512,2048]{1,0:T(8,128)(2,1)S(1)} %copy-done), kind=kOutput, calls=%fused_computation.15 | convolution fusion | flops 1078984704 | bytes 8912896 | tf_op jit(solution)/shard_map/vmap(jvp())/dot_general | solution.py:21
  24.3 1.4 copy-done.3
  25.7 1.1 fusion.65
  26.8 0.2 copy.28
  27.0 0.0 copy-start.7
  27.1 1.4 copy.29
  28.5 0.0 copy-start.9
  28.5 2.3 %copy.27 = bf16[2,256,512]{1,2,0:T(8,128)(2,1)} copy(bf16[2,256,512]{2,1,0:T(8,128)(2,1)} %get-tuple-element.8) | data formatting | bytes 1048576 | tf_op jit(solution)/shard_map/vmap(jvp())/split | solution.py:23
  30.8 0.1 and_convert_fusion
  30.9 0.0 copy-start.11
  30.9 0.0 copy-start.5
  30.9 3.6 %divide_convert_fusion = (bf16[2,8,256,256]{3,2,1,0:T(8,128)(2,1)S(1)}, f32[2,8,256,256]{3,2,1,0:T(8,128)}) fusion(f32[2]{0:T(128)S(1)} %convert_element_type.98, f32[2,256,256]{2,1,0:T(8,128)S(1)} %and_convert_fusion, bf16[2,256,8,64]{1,3,2,0:T(8,128)(2,1)S(1)} %bitcast.82, bf16[2,256,8,64]{1,3,2,0:T(8,128)(2,1)S(1)} %bitcast.84), kind=kOutput, calls=%fused_computation.13 | convolution fusion | flops 142606336 | bytes 7864328 | tf_op jit(solution)/shard_map/vmap(jvp(qhd,khd->hqk))/dot_general | solution.py:27
  34.5 0.0 copy-done.7
  34.5 0.0 copy-done.9
  34.5 0.0 copy-done.11
  34.5 1.3 copy-done.2
  35.8 0.0 copy-done.5
  35.8 0.8 bitcast_reduce_fusion
  36.6 1.4 copy.30
  38.0 0.1 fusion.43
  38.1 2.4 %multiply_reduce_fusion = (f32[2,256]{1,0:T(2,128)S(1)}, bf16[2,256,512]{2,1,0:T(8,128)(2,1)S(1)}) fusion(f32[2,256,512]{2,1,0:T(8,128)} %copy.30, f32[2,256]{1,0:T(2,128)S(1)} %broadcast_multiply_fusion, bf16[2,256,2048]{2,1,0:T(8,128)(2,1)} %copy-done.3, bf16[512,512]{1,0:T(8,128)(2,1)} %param.14, bf16[2,256,512]{2,1,0:T(8,128)(2,1)} %param.10, ...), kind=kOutput, calls=%fused_computation.46 | convolution fusion | flops 270794240 | bytes 3151872 | tf_op jit(solution)/shard_map/vmap(transpose(jvp()))/dot_general | solution.py:43
  40.6 0.0 copy-done.1
  40.6 0.1 copy-done.4
  40.7 1.4 fusion.41
  42.1 0.4 broadcast_add_fusion
  42.5 1.1 copy.31
  43.5 2.2 %fusion.68 = bf16[2,8,64,256]{3,2,1,0:T(8,128)(2,1)S(1)} fusion(bf16[2,8,64,256]{3,2,1,0:T(8,128)(2,1)} %bitcast.87, bf16[2,8,256,256]{3,2,1,0:T(8,128)(2,1)} %copy-done.2), kind=kOutput, calls=%fused_computation.105 | convolution fusion | flops 134217728 | bytes 3145728 | tf_op jit(solution)/shard_map/vmap(transpose(jvp(hqk,khd->qhd)))/dot_general | solution.py:37
  45.8 0.0 copy-done.6
  45.8 0.0 copy-start.10
  45.8 0.0 copy-start.8
  45.8 4.5 %fusion.7 = bf16[2,8,256,256]{3,2,1,0:T(8,128)(2,1)S(1)} fusion(f32[2,8,256,256]{3,2,1,0:T(8,128)} %get-tuple-element.20, f32[2]{0:T(128)S(1)} %convert_element_type.98, f32[2,256,256]{2,1,0:T(8,128)} %copy-done.11, bf16[2,8,64,256]{3,2,1,0:T(8,128)(2,1)} %bitcast.88, bf16[2,256,8,64]{1,3,2,0:T(8,128)(2,1)S(1)} %bitcast.81), kind=kOutput, calls=%fused_computation.12 | convolution fusion | flops 149946368 | bytes 7864328 | tf_op jit(solution)/shard_map/vmap(transpose(jvp(hqk,khd->qhd)))/dot_general | solution.py:37
  50.4 0.0 copy-done.10
  50.4 0.8 fusion.67
  51.1 0.0 copy-done.8
  51.1 1.3 fusion.66
  52.4 1.0 copy.32
  53.4 0.2 copy.33
  53.6 1.3 copy.34
  54.9 5.3 %fusion.36 = bf16[2,256,512]{2,1,0:T(8,128)(2,1)} fusion(bf16[512,2048]{1,0:T(8,128)(2,1)S(1)} %copy-done, f32[2,256,2048]{2,1,0:T(8,128)} %get-tuple-element.18, bf16[2,256,512]{2,1,0:T(8,128)(2,1)S(1)} %copy.34, bf16[2,256,512]{2,1,0:T(8,128)(2,1)S(1)} %copy.33, bf16[2,256,512]{2,1,0:T(8,128)(2,1)} %copy.32, bf16[2,256,512]{2,1,0:T(8,128)(2,1)} %get-tuple-element.11, ...), kind=kOutput, calls=%fused_computation.36 | convolution fusion | flops 1093140480 | bytes 9439232 | tf_op jit(solution)/shard_map/vmap(transpose(jvp()))/dot_general | solution.py:21
  60.2 4.2 %scatter_custom_fusion.1 = bf16[1024,512]{1,0:T(8,128)(2,1)} fusion(s32[512]{0:T(512)S(1)} %bitcast.96, bf16[512,512]{1,0:T(8,128)(2,1)} %bitcast.98, bf16[]{:T(256)} %constant.91.clone.1), kind=kCustom, calls=%fused_computation.51 | custom fusion | bytes 1049088 | tf_op jit(solution)/shard_map/scatter | solution.py:73
  64.4 0.0 all-to-all-done
  64.4 3.5 %all-to-all-start.1 = ((bf16[4,256,512]{2,1,0:T(8,128)(2,1)}), bf16[4,256,512]{2,1,0:T(8,128)(2,1)S(1)}, u32[]{:S(2)}, u32[]{:S(2)}) async-start(bf16[4,256,512]{2,1,0:T(8,128)(2,1)} %bitcast.23), calls=%async_computation.1 | async-start | bytes 2097152 | tf_op jit(solution)/shard_map/all_to_all | solution.py:111
  67.9 0.0 reduce-scatter.2.cloned.1.call-start
  68.0 14.3 %all-to-all-done.1 = bf16[4,256,512]{2,1,0:T(8,128)(2,1)S(1)} async-done(((bf16[4,256,512]{2,1,0:T(8,128)(2,1)}), bf16[4,256,512]{2,1,0:T(8,128)(2,1)S(1)}, u32[]{:S(2)}, u32[]{:S(2)}) %all-to-all-start.1) | async-done | bytes 1048608 | tf_op jit(solution)/shard_map/all_to_all | solution.py:111
  82.3 7.5 %scatter_custom_fusion.2 = f32[256,512]{1,0:T(8,128)} fusion(s32[1024]{0:T(1024)S(1)} %bitcast.94, bf16[1024,512]{1,0:T(8,128)(2,1)S(1)} %bitcast.79, f32[]{:T(128)} %constant.78.clone.1), kind=kCustom, calls=%fused_computation.24 | custom fusion | flops 1048576 | bytes 1572868 | tf_op jit(solution)/shard_map/scatter-add | solution.py:90
  89.8 1.8 %convert_element_type.118 = bf16[256,512]{1,0:T(8,128)(2,1)} convert(f32[256,512]{1,0:T(8,128)} %scatter_custom_fusion.2) | non-fusion elementwise | flops 131072 | bytes 786432 | tf_op jit(solution)/shard_map/convert_element_type | solution.py:116
  91.6 0.0 reduce-scatter.2.cloned.1.call-update
  91.6 63.6 %reduce-scatter.2.cloned.1.call-done = bf16[32,512]{1,0:T(8,128)(2,1)} async-done(((bf16[256,512]{1,0:T(8,128)(2,1)}), bf16[32,512]{1,0:T(8,128)(2,1)}) %reduce-scatter.2.cloned.1.call-update) | async-done | bytes 32784 | tf_op jit(solution)/shard_map/reduce_scatter | solution.py:115
  155.2 0.9 fusion.52
  156.1 0.0 copy-done.12
  156.1 1.5 divide_subtract_fusion
  (27 shorter events, 0.2 us)
Async XLA Ops:
  7.2 12.6 %copy-start = (bf16[512,2048]{1,0:T(8,128)(2,1)S(1)}, bf16[512,2048]{1,0:T(8,128)(2,1)}, u32[]{:S(2)}) copy-start(bf16[512,2048]{1,0:T(8,128)(2,1)} %param.13) | copy-start | bytes 6291460
  14.1 50.3 %all-to-all-start = ((s32[4,1,256]{2,1,0:T(1,128)}), s32[4,1,256]{2,1,0:T(1,128)S(1)}, u32[]{:S(2)}, u32[]{:S(2)}) async-start(s32[4,1,256]{2,1,0:T(1,128)} %bitcast.3), calls=%async_computation | async-start | bytes 8192 | tf_op jit(solution)/shard_map/all_to_all | solution.py:112
  24.3 1.4 copy-start.3
  27.0 7.5 %copy-start.7 = (bf16[2,256,512]{1,2,0:T(8,128)(2,1)}, bf16[2,256,512]{1,2,0:T(8,128)(2,1)S(1)}, u32[]{:S(2)}) copy-start(bf16[2,256,512]{1,2,0:T(8,128)(2,1)S(1)} %copy.28) | copy-start | bytes 1572868
  28.5 6.0 %copy-start.9 = (bf16[2,256,512]{1,2,0:T(8,128)(2,1)}, bf16[2,256,512]{1,2,0:T(8,128)(2,1)S(1)}, u32[]{:S(2)}) copy-start(bf16[2,256,512]{1,2,0:T(8,128)(2,1)S(1)} %copy.29) | copy-start | bytes 1572868
  30.9 3.6 %copy-start.11 = (f32[2,256,256]{2,1,0:T(8,128)}, f32[2,256,256]{2,1,0:T(8,128)S(1)}, u32[]{:S(2)}) copy-start(f32[2,256,256]{2,1,0:T(8,128)S(1)} %and_convert_fusion) | copy-start | bytes 1572868
  30.9 4.9 %copy-start.5 = (bf16[2,256,512]{1,2,0:T(8,128)(2,1)S(1)}, bf16[2,256,512]{1,2,0:T(8,128)(2,1)}, u32[]{:S(2)}) copy-start(bf16[2,256,512]{1,2,0:T(8,128)(2,1)} %copy.27) | copy-start | bytes 1572868
  34.5 1.3 copy-start.2
  38.0 2.6 %copy-start.1 = (f32[2,256,512]{2,1,0:T(8,128)S(1)}, f32[2,256,512]{2,1,0:T(8,128)}, u32[]{:S(2)}) copy-start(f32[2,256,512]{2,1,0:T(8,128)} %copy.30) | copy-start | bytes 3145732
  38.0 2.7 %copy-start.4 = (bf16[2,256,2048]{2,1,0:T(8,128)(2,1)S(1)}, bf16[2,256,2048]{2,1,0:T(8,128)(2,1)}, u32[]{:S(2)}) copy-start(bf16[2,256,2048]{2,1,0:T(8,128)(2,1)} %copy-done.3) | copy-start | bytes 6291460
  40.7 5.1 %copy-start.6 = (bf16[2,256,512]{1,2,0:T(8,128)(2,1)S(1)}, bf16[2,256,512]{1,2,0:T(8,128)(2,1)}, u32[]{:S(2)}) copy-start(bf16[2,256,512]{1,2,0:T(8,128)(2,1)} %copy.27) | copy-start | bytes 1572868
  45.8 4.6 %copy-start.10 = (bf16[2,256,512]{1,2,0:T(8,128)(2,1)S(1)}, bf16[2,256,512]{1,2,0:T(8,128)(2,1)}, u32[]{:S(2)}) copy-start(bf16[2,256,512]{1,2,0:T(8,128)(2,1)} %copy-done.9) | copy-start | bytes 1572868
  45.8 5.3 %copy-start.8 = (bf16[2,256,512]{1,2,0:T(8,128)(2,1)S(1)}, bf16[2,256,512]{1,2,0:T(8,128)(2,1)}, u32[]{:S(2)}) copy-start(bf16[2,256,512]{1,2,0:T(8,128)(2,1)} %copy-done.7) | copy-start | bytes 1572868
  60.2 95.9 %copy-start.12 = (f32[32,512]{1,0:T(8,128)S(1)}, f32[32,512]{1,0:T(8,128)}, u32[]{:S(2)}) copy-start(f32[32,512]{1,0:T(8,128)} %param.15) | copy-start | bytes 196612
  60.2 95.9 %copy-start.13 = (f32[32,512]{1,0:T(8,128)S(1)}, f32[32,512]{1,0:T(8,128)}, u32[]{:S(2)}) copy-start(f32[32,512]{1,0:T(8,128)} %param.16) | copy-start | bytes 196612
  60.2 95.9 %copy-start.14 = (f32[32,512]{1,0:T(8,128)S(1)}, f32[32,512]{1,0:T(8,128)}, u32[]{:S(2)}) copy-start(f32[32,512]{1,0:T(8,128)} %param.17) | copy-start | bytes 196612
  64.4 17.9 %all-to-all-start.1 = ((bf16[4,256,512]{2,1,0:T(8,128)(2,1)}), bf16[4,256,512]{2,1,0:T(8,128)(2,1)S(1)}, u32[]{:S(2)}, u32[]{:S(2)}) async-start(bf16[4,256,512]{2,1,0:T(8,128)(2,1)} %bitcast.23), calls=%async_computation.1 | async-start | bytes 2097152 | tf_op jit(solution)/shard_map/all_to_all | solution.py:111
  67.9 87.3 %reduce-scatter.2.cloned.1.call-start = ((), (), s32[]{:S(2)}) async-start(), calls=%async_computation.3 | async-start | bytes 294912 | tf_op jit(solution)/shard_map/reduce_scatter | solution.py:115
Sparse Core Ops, SparseCore 0:
  91.7 63.4 reduce-scatter.1
where the time goes:
time: 165 us
  waiting for transfers between devices  78 us (47%)
  matrix products  25.5 us (15%)
  local copies, waits for them, and re-layouts  20.3 us (12%)
  other arithmetic  18.7 us (11%)
  between operations  14.3 us (9%)
  starting transfers between devices  7.82 us (5%)
    reduce_scatter x1, waiting for transfers between devices, on_device(): lax.psum_scatter(row_grad.astype(jnp.bfloat16), 'wide', scatter_dimension...  63.6 us
    all_to_all x1, waiting for transfers between devices, on_device(): lax.all_to_all(outgoing, 'narrow', split_axis=0, concat_axis=0, tiled=True)  14.3 us
    dot_general x2, matrix products, layer_forward(): jnp.dot(source.astype(jnp.bfloat16), w_in, preferred_element_type=jnp.flo...  9.9 us
    dot_general x3, matrix products, layer_forward(): jnp.einsum('hqk,khd->qhd', attention, value_part, preferred_element_type=...  7.55 us
    scatter-add x1, other arithmetic, owner_total(): return empty.at[flat_labels].add(row_data.astype(jnp.float32), mode='drop')  7.49 us
    dot_general x3, matrix products, layer_forward(): jnp.einsum('qhd,khd->hqk', query_part, key_part, preferred_element_type=j...  5.65 us
    split x4, local copies, waits for them, and re-layouts, layer_forward(): gate_part, value_part, query_part, key_part = jnp.split(hidden, 4, axis=1)  5.01 us
    all_to_all x1, starting transfers between devices, on_device(): lax.all_to_all(labels, 'narrow', split_axis=0, concat_axis=0, tiled=True)  4.26 us
  transfers between devices with their start and end apart: 3, of which 2 were waited for; matrix products, arithmetic and copies ran while one was open for 26% of the time, Pallas kernels for 0%

commit v1 on v0

v1 whole, which is shorter than its diff:
```python
import functools

import jax
import jax.numpy as jnp
from jax import lax
from jax.experimental import pallas as pl
from jax.experimental.pallas import tpu as pltpu
from jax.sharding import PartitionSpec as P

HEADS = 8
CORES = 2
LANES = 128

norm_eps = 1e-06
clip_norm = 4.0
learn_rate = 0.5
beta_first = 0.9
beta_second = 0.999
adam_step = 3.0
adam_eps = 1e-08

AXES = ("wide", "narrow")


def layout_of(wide, narrow):
    cores = CORES if narrow % CORES == 0 else 1
    inner = 2 if wide % 2 == 0 else 1
    return cores, inner, narrow // cores, wide // inner


def destination(wide, narrow, w, n, cr, ir, yr, zr):
    cores, inner, pairs, outer = layout_of(wide, narrow)
    z, i = w // inner, w % inner
    y, c = n // cores, n % cores
    w_to = ((z + zr) % outer) * inner + (i + ir) % inner
    n_to = ((y + yr) % pairs) * cores + (c + cr) % cores
    return w_to, n_to


def send(x, wide, narrow, offset):
    perm = []
    for w in range(wide):
        for n in range(narrow):
            w_to, n_to = destination(wide, narrow, w, n, *offset)
            perm.append((w * narrow + n, w_to * narrow + n_to))
    return lax.ppermute(x, AXES, perm)


def dot(a, b):
    return lax.dot_general(a, b, (((1,), (0,)), ((), ())), preferred_element_type=jnp.float32)


def dot_nt(a, b):
    return lax.dot_general(a, b, (((1,), (1,)), ((), ())), preferred_element_type=jnp.float32)


def sigmoid(x):
    return 1.0 / (1.0 + jnp.exp(-x))


def local_kernel(
    wide, narrow, rows_dev,
    len_ref, rows_ref, tok_ref, cot_ref, win_ref, wout_ref,
    part_ref,
    hid, slope, att, fac, mixed, inner_grad, dgated, grads, dm_t, q_t, dk_t, dv_t,
):
    micro, lmax, width = tok_ref.shape
    half = lmax // 2
    per_head = width // HEADS
    f32, bf16 = jnp.float32, jnp.bfloat16
    total = micro * lmax

    source = tok_ref[...].reshape(total, width)
    tile = 256
    for t in range(4 * width // tile):
        cols = pl.ds(t * tile, tile)
        inner = dot(source, win_ref[:, cols])
        gate_s = sigmoid(inner)
        act = inner * gate_s
        hid[:, cols] = act.astype(bf16)
        slope[:, cols] = gate_s + act * (1.0 - gate_s)

    row = lax.broadcasted_iota(jnp.int32, (lmax, 1), 0)
    for s in range(micro):
        live = (row < len_ref[s]).astype(f32)
        masked = (cot_ref[s].astype(f32) * live).astype(bf16)
        grads[pl.ds(s * lmax, lmax), :] = masked
    dgated[...] = dot_nt(grads[...], wout_ref[...]).astype(bf16)

    lane = lax.broadcasted_iota(jnp.int32, (1, LANES), 1)
    heads_here = LANES // per_head
    masks = [((lane // per_head) == h).astype(bf16) for h in range(heads_here)]
    scale = per_head ** (-0.5)
    causal = lax.broadcasted_iota(jnp.int32, (half, half), 1) <= lax.broadcasted_iota(jnp.int32, (half, half), 0)
    none = jnp.zeros((half, half), bf16)

    def one_sequence(s, carry):
        base = pl.multiple_of(s * lmax, lmax)
        here = pl.ds(base, lmax)
        length = len_ref[s]
        share = jnp.where(row < length, 1.0 / jnp.full((lmax, 1), length, jnp.int32).astype(f32), 0.0)

        for p in range(width // LANES):
            q = hid[here, pl.ds(2 * width + p * LANES, LANES)]
            k = hid[here, pl.ds(3 * width + p * LANES, LANES)]
            v = hid[here, pl.ds(width + p * LANES, LANES)]
            weights, values = [], []
            for h in range(heads_here):
                head = p * heads_here + h
                qm = q * (masks[h] * jnp.asarray(scale, bf16))
                parts = []
                for b in range(2):
                    rows = slice(b * half, (b + 1) * half)
                    score = dot_nt(qm[rows], k[: (b + 1) * half])
                    gate_s = sigmoid(score)
                    act = score * gate_s
                    part = share[rows]
                    if b == 0:
                        w_b = jnp.where(causal, act * part, 0.0)
                        f_b = jnp.where(causal, (gate_s + act * (1.0 - gate_s)) * (part * scale), 0.0)
                        fac[head, :half, :half] = f_b
                        parts.append(jnp.concatenate([w_b.astype(bf16), none], axis=1))
                    else:
                        w_b = act * part
                        f_b = (gate_s + act * (1.0 - gate_s)) * (part * scale)
                        fac[head, half:, :half] = f_b[:, :half]
                        fac[head, half:, half:] = jnp.where(causal, f_b[:, half:], 0.0)
                        parts.append(
                            jnp.concatenate(
                                [w_b[:, :half].astype(bf16), jnp.where(causal, w_b[:, half:], 0.0).astype(bf16)], axis=1
                            )
                        )
                weight = jnp.concatenate(parts, axis=0)
                att[head] = weight
                weights.append(weight)
                values.append(v * masks[h])
            mixed[:, pl.ds(p * LANES, LANES)] = dot(
                jnp.concatenate(weights, axis=1), jnp.concatenate(values, axis=0)
            )

        mix = mixed[...]
        centered = mix - jnp.mean(mix, axis=1, keepdims=True)
        inv = lax.rsqrt(jnp.mean(centered * centered, axis=1, keepdims=True) + norm_eps)
        normed = centered * inv
        dg = dgated[here, :].astype(f32)
        gate = hid[here, pl.ds(0, width)].astype(f32)
        dgate = (dg * normed).astype(bf16).astype(f32)
        inner_grad[here, pl.ds(0, width)] = (dgate * slope[here, pl.ds(0, width)]).astype(bf16)
        dn = dg * gate
        dmix = inv * (
            dn - jnp.mean(dn, axis=1, keepdims=True) - normed * jnp.mean(dn * normed, axis=1, keepdims=True)
        )
        dm = dmix.astype(bf16)
        dm_t[...] = dm.T
        q_t[...] = hid[here, pl.ds(2 * width, width)].T

        for p in range(width // LANES):
            k = hid[here, pl.ds(3 * width + p * LANES, LANES)]
            v = hid[here, pl.ds(width + p * LANES, LANES)]
            dmp = dm[:, p * LANES : (p + 1) * LANES]
            scores, keys = [], []
            for h in range(heads_here):
                head = p * heads_here + h
                dmm = dmp * masks[h]
                d_top = dot_nt(dmm[:half], v[:half]).astype(bf16).astype(f32)
                d_low = dot_nt(dmm[half:], v).astype(bf16).astype(f32)
                ds_top = (d_top * fac[head, :half, :half]).astype(bf16)
                ds_low = (d_low * fac[head, half:, :]).astype(bf16)
                ds = jnp.concatenate([jnp.concatenate([ds_top, none], axis=1), ds_low], axis=0)
                scores.append(ds)
                keys.append(k * masks[h])
                feat = pl.ds(head * per_head, per_head)
                dk_t[feat, :] = dot(q_t[feat, :], ds).astype(bf16)
                dv_t[feat, :] = dot(dm_t[feat, :], att[head]).astype(bf16)
            dq = dot(jnp.concatenate(scores, axis=1), jnp.concatenate(keys, axis=0)).astype(bf16).astype(f32)
            cols = pl.ds(2 * width + p * LANES, LANES)
            inner_grad[here, cols] = (dq * slope[here, cols]).astype(bf16)
        for part, source_t in ((1, dv_t), (3, dk_t)):
            cols = pl.ds(part * width, width)
            inner_grad[here, cols] = (source_t[...].T.astype(f32) * slope[here, cols]).astype(bf16)
        return carry

    lax.fori_loop(0, micro, one_sequence, 0)

    back = dot_nt(inner_grad[...], win_ref[...]).astype(bf16).astype(f32)
    grads[...] = (back + grads[...].astype(f32)).astype(bf16)

    cores, inner_w, pairs, outer = layout_of(wide, narrow)
    w_me, n_me = lax.axis_index("wide"), lax.axis_index("narrow")
    z_me, i_me = w_me // inner_w, w_me % inner_w
    y_me, c_me = n_me // cores, n_me % cores
    per_chunk = 8
    slot = lax.broadcasted_iota(jnp.int32, (rows_dev, lmax), 0)

    def one_chunk(j, carry):
        pieces = []
        for b in range(per_chunk):
            block = j * per_chunk + b
            zr = block % outer
            yr = (block // outer) % pairs
            ir = (block // (outer * pairs)) % inner_w
            cr = block // (outer * pairs * inner_w)
            w_to = ((z_me + zr) % outer) * inner_w + (i_me + ir) % inner_w
            n_to = ((y_me + yr) % pairs) * cores + (c_me + cr) % cores
            first = (w_to * narrow + n_to) * rows_dev
            want = slot + first
            pieces.append(
                jnp.concatenate(
                    [(want == rows_ref[s : s + 1, :]).astype(f32).astype(bf16) for s in range(micro)], axis=1
                )
            )
        chosen = jnp.concatenate(pieces, axis=0)
        size = per_chunk * rows_dev
        part_ref[pl.ds(pl.multiple_of(j * size, size), size), :] = dot(chosen, grads[...]).astype(bf16)
        return carry

    chunks = wide * narrow // per_chunk
    lax.fori_loop(0, chunks, one_chunk, 0)


def local_rows(wide, narrow, rows_dev, tokens, cotangent, lengths, item_rows, w_in, w_out):
    micro, lmax, width = tokens.shape
    total = micro * lmax
    items = wide * narrow * rows_dev
    f32, bf16 = jnp.float32, jnp.bfloat16
    vmem = pl.BlockSpec(memory_space=pltpu.VMEM)
    return pl.pallas_call(
        functools.partial(local_kernel, wide, narrow, rows_dev),
        out_shape=jax.ShapeDtypeStruct((items, width), bf16),
        in_specs=[pl.BlockSpec(memory_space=pltpu.SMEM)] + [vmem] * 5,
        out_specs=vmem,
        scratch_shapes=[
            pltpu.VMEM((total, 4 * width), bf16),
            pltpu.VMEM((total, 4 * width), f32),
            pltpu.VMEM((HEADS, lmax, lmax), bf16),
            pltpu.VMEM((HEADS, lmax, lmax), f32),
            pltpu.VMEM((lmax, width), f32),
            pltpu.VMEM((total, 4 * width), bf16),
            pltpu.VMEM((total, width), bf16),
            pltpu.VMEM((total, width), bf16),
            pltpu.VMEM((width, lmax), bf16),
            pltpu.VMEM((width, lmax), bf16),
            pltpu.VMEM((width, lmax), bf16),
            pltpu.VMEM((width, lmax), bf16),
        ],
        cost_estimate=pl.CostEstimate(
            flops=16 * total * width * width + 12 * total * lmax * width,
            bytes_accessed=4 * total * width + 10 * width * width + 2 * items * width,
            transcendentals=HEADS * total * lmax,
        ),
        name="local_rows",
    )(lengths, item_rows, tokens, cotangent, w_in, w_out)


def adam_rows(row_grad, table, moment_one, moment_two):
    row_norms = jnp.sqrt(jnp.sum(row_grad * row_grad, axis=1, keepdims=True))
    clipped = row_grad * (clip_norm / jnp.maximum(row_norms, clip_norm))
    first_moment = beta_first * moment_one + (1.0 - beta_first) * clipped
    second_moment = beta_second * moment_two + (1.0 - beta_second) * clipped * clipped
    step_size = learn_rate / (1.0 - beta_first**adam_step)
    scaled = jnp.sqrt(second_moment / (1.0 - beta_second**adam_step)) + adam_eps
    return (table - step_size * first_moment / scaled, first_moment, second_moment)


def gather_sum(x, offsets, wide, narrow):
    arrived = [send(x[k], wide, narrow, offsets[k]) for k in range(1, len(offsets))]
    out = x[0].astype(jnp.float32)
    for piece in arrived:
        out = out + piece.astype(jnp.float32)
    return out


def on_device(tokens, cotangent, lengths, item_rows, w_in, w_out, table, moment_one, moment_two):
    wide, narrow = lax.axis_size("wide"), lax.axis_size("narrow")
    rows_dev, width = table.shape
    cores, inner, pairs, outer = layout_of(wide, narrow)
    partial = local_rows(wide, narrow, rows_dev, tokens, cotangent, lengths, item_rows, w_in, w_out)
    stages = (
        [(c, 0, 0, 0) for c in range(cores)],
        [(0, i, y, 0) for i in range(inner) for y in range(pairs)],
        [(0, 0, 0, z) for z in range(outer)],
    )
    held = partial
    for offsets in stages:
        held = held.astype(jnp.bfloat16).reshape(len(offsets), -1, width)
        held = gather_sum(held, offsets, wide, narrow)
    return adam_rows(held, table, moment_one, moment_two)


def solution(mesh):
    return jax.shard_map(
        on_device,
        mesh=mesh,
        in_specs=(
            P(AXES, None, None),
            P(AXES, None, None),
            P(AXES),
            P(AXES, None),
            P(),
            P(),
            P(AXES, None),
            P(AXES, None),
            P(AXES, None),
        ),
        out_specs=(P(AXES, None), P(AXES, None), P(AXES, None)),
        check_vma=False,
    )
```

time: 165 us -> 41.1 us (0.25)
  waiting for transfers between devices: 78 us -> 11.8 us
  matrix products: 25.5 us -> 0 us
  local copies, waits for them, and re-layouts: 20.3 us -> 1.16 us
  other arithmetic: 18.7 us -> 2.16 us
  Pallas kernels: 0 us -> 15.3 us
  between operations: 14.3 us -> 0.69 us
  starting transfers between devices: 7.82 us -> 9.85 us
    reduce_scatter x1 -> x0, waiting for transfers between devices: 63.6 us -> none  [on_device(): lax.psum_scatter(row_grad.astype(jnp.bfloat16), 'wide', scatter_dimension...]
    dot_general x9 -> x0, matrix products: 25.5 us -> none  [the longest x2 9.9 us: layer_forward(): jnp.dot(source.astype(jnp.bfloat16), w_in, preferred_element_type=jnp.flo...]
    pallas_call x0 -> x1, Pallas kernels: none -> 15.3 us  [local_rows(): pl.pallas_call(functools.partial(local_kernel, wide, narrow, rows_dev), o...]
    all_to_all x2 -> x0, waiting for transfers between devices: 14.3 us -> none  [the longest x1 14.3 us: on_device(): lax.all_to_all(outgoing, 'narrow', split_axis=0, concat_axis=0, tiled=True)]
    ppermute x0 -> x7, waiting for transfers between devices: none -> 11.8 us  [send(): return lax.ppermute(x, AXES, perm)]
    ppermute x0 -> x7, starting transfers between devices: none -> 9.85 us  [send(): return lax.ppermute(x, AXES, perm)]
    all_to_all x2 -> x0, starting transfers between devices: 7.78 us -> none  [the longest x1 4.26 us: on_device(): lax.all_to_all(labels, 'narrow', split_axis=0, concat_axis=0, tiled=True)]
    scatter-add x1 -> x0, other arithmetic: 7.49 us -> none  [owner_total(): return empty.at[flat_labels].add(row_data.astype(jnp.float32), mode='drop')]
  transfers between devices with their start and end apart: 3 -> 7, of which waited for: 2 -> 6; matrix products, arithmetic and copies ran while one was open for 26% -> 0% of each run, Pallas kernels for 0% -> 0%
where the time goes in v1:
time: 41.1 us; the launch traced here: 40.9 us
  Pallas kernels  15.3 us (37%)
  waiting for transfers between devices  11.8 us (29%)
  starting transfers between devices  9.85 us (24%)
  other arithmetic  2.16 us (5%)
  local copies, waits for them, and re-layouts  1.16 us (3%)
  between operations  0.69 us (2%)
    pallas_call x1, Pallas kernels, local_rows(): pl.pallas_call(functools.partial(local_kernel, wide, narrow, rows_dev), o...  15.3 us
    ppermute x7, waiting for transfers between devices, send(): return lax.ppermute(x, AXES, perm)  11.8 us
    ppermute x7, starting transfers between devices, send(): return lax.ppermute(x, AXES, perm)  9.85 us
    convert_element_type x2, other arithmetic, on_device(): held = held.astype(jnp.bfloat16).reshape(len(offsets), -1, width)  1.24 us
    slice x3, local copies, waits for them, and re-layouts, gather_sum(): x[k]  1.15 us
  transfers between devices with their start and end apart: 7, of which 6 were waited for; matrix products, arithmetic and copies ran while one was open for 0% of the time, Pallas kernels for 0%

profile of v1, /device:TPU:0, one launch (start us, length us, event | category | flops | bytes accessed | tf_op | source)
XLA Modules:
  0.0 40.9 jit_solution(12881466821496835899)
XLA Ops:
  0.6 15.3 %local_rows.1 = bf16[1024,512]{1,0:T(8,128)(2,1)} custom-call(s32[2]{0:T(128)} %len_ref.1, s32[2,256]{1,0:T(2,128)} %rows_ref.1, bf16[2,256,512]{2,1,0:T(8,128)(2,1)} %tok_ref.1, bf16[2,256,512]{2,1,0:T(8,128)(2,1)} %cot_ref.1, bf16[512,2048]{1,0:T(8,128)(2,1)} %win_ref.1, bf16[512,512]{1,0:T(8,128)(2,1)} %wout_ref.1), custom_call_target="tpu_custom_call" | custom-call | flops 2952790016 | bytes 4718592 | tf_op jit(solution)/shard_map/local_rows/pallas_call | solution.py:227
  15.9 0.0 copy-start
  15.9 0.0 copy-start.1
  15.9 0.0 copy-start.2
  15.9 1.1 %slice.51 = bf16[512,512]{1,0:T(8,128)(2,1)S(1)} slice(bf16[1024,512]{1,0:T(8,128)(2,1)} %local_rows.1), slice={[512:1024], [0:512]} | slice | bytes 1048576 | tf_op jit(solution)/shard_map/slice | solution.py:266
  17.0 0.6 %collective-permute-start = (bf16[512,512]{1,0:T(8,128)(2,1)S(1)}, bf16[512,512]{1,0:T(8,128)(2,1)S(1)}, u32[]{:S(2)}, u32[]{:S(2)}) collective-permute-start(bf16[512,512]{1,0:T(8,128)(2,1)S(1)} %slice.51), channel_id=1, source_target_pairs={{0,1},{1,0},{2,3},{3,2},{4,5},{5,4},{6,7},{7,6},{8,9},{9,8},{10,11... | collective-permute-start | bytes 1572872 | tf_op jit(solution)/shard_map/ppermute | solution.py:46
  17.6 1.5 %collective-permute-done = bf16[512,512]{1,0:T(8,128)(2,1)S(1)} collective-permute-done((bf16[512,512]{1,0:T(8,128)(2,1)S(1)}, bf16[512,512]{1,0:T(8,128)(2,1)S(1)}, u32[]{:S(2)}, u32[]{:S(2)}) %collective-permute-start) | collective-permute-done | bytes 524320 | tf_op jit(solution)/shard_map/ppermute | solution.py:46
  19.1 1.2 %add_convert_fusion = bf16[512,512]{1,0:T(8,128)(2,1)S(1)} fusion(bf16[512,512]{1,0:T(8,128)(2,1)S(1)} %collective-permute-done, bf16[1024,512]{1,0:T(8,128)(2,1)} %local_rows.1), kind=kLoop, calls=%fused_computation | loop fusion | flops 1048576 | bytes 1572864 | tf_op jit(solution)/shard_map/convert_element_type | solution.py:285
  20.3 2.9 %collective-permute-start.1 = (bf16[128,512]{1,0:T(8,128)(2,1)S(1)}, bf16[128,512]{1,0:T(8,128)(2,1)S(1)}, u32[]{:S(2)}, u32[]{:S(2)}) collective-permute-start(bf16[128,512]{1,0:T(8,128)(2,1)S(1)} %get-tuple-element.6), channel_id=1, source_target_pairs={{0,2},{1,3},{2,0},{3,1},{4,6},{5,7},{6,4},{7,5},{8,10},{9,11},{10,... | collective-permute-start | bytes 393224 | tf_op jit(solution)/shard_map/ppermute | solution.py:46
  23.3 1.4 %collective-permute-start.3 = (bf16[128,512]{1,0:T(8,128)(2,1)S(1)}, bf16[128,512]{1,0:T(8,128)(2,1)S(1)}, u32[]{:S(2)}, u32[]{:S(2)}) collective-permute-start(bf16[128,512]{1,0:T(8,128)(2,1)S(1)} %get-tuple-element.7), channel_id=1, source_target_pairs={{0,6},{1,7},{2,4},{3,5},{4,2},{5,3},{6,0},{7,1},{8,14},{9,15},{10,... | collective-permute-start | bytes 393224 | tf_op jit(solution)/shard_map/ppermute | solution.py:46
  24.7 0.1 collective-permute-start.2
  24.8 4.4 %collective-permute-done.1 = bf16[128,512]{1,0:T(8,128)(2,1)S(1)} collective-permute-done((bf16[128,512]{1,0:T(8,128)(2,1)S(1)}, bf16[128,512]{1,0:T(8,128)(2,1)S(1)}, u32[]{:S(2)}, u32[]{:S(2)}) %collective-permute-start.1) | collective-permute-done | bytes 131104 | tf_op jit(solution)/shard_map/ppermute | solution.py:46
  29.2 1.3 %collective-permute-done.3 = bf16[128,512]{1,0:T(8,128)(2,1)S(1)} collective-permute-done((bf16[128,512]{1,0:T(8,128)(2,1)S(1)}, bf16[128,512]{1,0:T(8,128)(2,1)S(1)}, u32[]{:S(2)}, u32[]{:S(2)}) %collective-permute-start.3) | collective-permute-done | bytes 131104 | tf_op jit(solution)/shard_map/ppermute | solution.py:46
  30.6 0.6 %collective-permute-done.2 = bf16[128,512]{1,0:T(8,128)(2,1)S(1)} collective-permute-done((bf16[128,512]{1,0:T(8,128)(2,1)S(1)}, bf16[128,512]{1,0:T(8,128)(2,1)S(1)}, u32[]{:S(2)}, u32[]{:S(2)}) %collective-permute-start.2) | collective-permute-done | bytes 131104 | tf_op jit(solution)/shard_map/ppermute | solution.py:46
  31.2 0.1 add_convert_fusion.1
  31.3 1.8 %collective-permute-start.4 = (bf16[32,512]{1,0:T(8,128)(2,1)S(1)}, bf16[32,512]{1,0:T(8,128)(2,1)S(1)}, u32[]{:S(2)}, u32[]{:S(2)}) collective-permute-start(bf16[32,512]{1,0:T(8,128)(2,1)S(1)} %get-tuple-element.9), channel_id=1, source_target_pairs={{0,8},{1,9},{2,10},{3,11},{4,12},{5,13},{6,14},{7,15},{8,16},{9,17... | collective-permute-start | bytes 98312 | tf_op jit(solution)/shard_map/ppermute | solution.py:46
  33.1 2.1 %collective-permute-start.6 = (bf16[32,512]{1,0:T(8,128)(2,1)S(1)}, bf16[32,512]{1,0:T(8,128)(2,1)S(1)}, u32[]{:S(2)}, u32[]{:S(2)}) collective-permute-start(bf16[32,512]{1,0:T(8,128)(2,1)S(1)} %get-tuple-element.10), channel_id=1, source_target_pairs={{0,24},{1,25},{2,26},{3,27},{4,28},{5,29},{6,30},{7,31},{8,0},{9,1... | collective-permute-start | bytes 98312 | tf_op jit(solution)/shard_map/ppermute | solution.py:46
  35.2 0.9 %collective-permute-start.5 = (bf16[32,512]{1,0:T(8,128)(2,1)S(1)}, bf16[32,512]{1,0:T(8,128)(2,1)S(1)}, u32[]{:S(2)}, u32[]{:S(2)}) collective-permute-start(bf16[32,512]{1,0:T(8,128)(2,1)S(1)} %get-tuple-element.11), channel_id=1, source_target_pairs={{0,16},{1,17},{2,18},{3,19},{4,20},{5,21},{6,22},{7,23},{8,24},{9,... | collective-permute-start | bytes 98312 | tf_op jit(solution)/shard_map/ppermute | solution.py:46
  36.1 1.3 %collective-permute-done.4 = bf16[32,512]{1,0:T(8,128)(2,1)S(1)} collective-permute-done((bf16[32,512]{1,0:T(8,128)(2,1)S(1)}, bf16[32,512]{1,0:T(8,128)(2,1)S(1)}, u32[]{:S(2)}, u32[]{:S(2)}) %collective-permute-start.4) | collective-permute-done | bytes 32800 | tf_op jit(solution)/shard_map/ppermute | solution.py:46
  37.4 0.0 collective-permute-done.6
  37.4 2.6 %collective-permute-done.5 = bf16[32,512]{1,0:T(8,128)(2,1)S(1)} collective-permute-done((bf16[32,512]{1,0:T(8,128)(2,1)S(1)}, bf16[32,512]{1,0:T(8,128)(2,1)S(1)}, u32[]{:S(2)}, u32[]{:S(2)}) %collective-permute-start.5) | collective-permute-done | bytes 32800 | tf_op jit(solution)/shard_map/ppermute | solution.py:46
  40.0 0.1 multiply_reduce_fusion
  40.1 0.0 copy-done
  40.1 0.0 copy-done.1
  40.1 0.0 copy-done.2
  40.2 0.8 %divide_subtract_fusion = (f32[32,512]{1,0:T(8,128)}, f32[32,512]{1,0:T(8,128)}, f32[32,512]{1,0:T(8,128)}) fusion(f32[32,512]{1,0:T(8,128)S(1)} %copy-done, f32[32]{0:T(128)S(1)} %maximum_divide_fusion, bf16[32,512]{1,0:T(8,128)(2,1)S(1)} %collective-permute-done.6, bf16[32,512]{1,0:T(8,128)(2,1)S(1)} %collective-permute-done.5, ...), kind=kLoop, calls=%fused_computation.4 | loop fusion | flops 327680 | bytes 524416 | tf_op jit(solution)/shard_map/sub | solution.py:262
  (3 shorter events, 0.0 us)
Async XLA Ops:
  15.9 24.2 %copy-start = (f32[32,512]{1,0:T(8,128)S(1)}, f32[32,512]{1,0:T(8,128)}, u32[]{:S(2)}) copy-start(f32[32,512]{1,0:T(8,128)} %param.15) | copy-start | bytes 196612
  15.9 24.2 %copy-start.1 = (f32[32,512]{1,0:T(8,128)S(1)}, f32[32,512]{1,0:T(8,128)}, u32[]{:S(2)}) copy-start(f32[32,512]{1,0:T(8,128)} %param.16) | copy-start | bytes 196612
  15.9 24.2 %copy-start.2 = (f32[32,512]{1,0:T(8,128)S(1)}, f32[32,512]{1,0:T(8,128)}, u32[]{:S(2)}) copy-start(f32[32,512]{1,0:T(8,128)} %param.17) | copy-start | bytes 196612
  17.0 2.1 %collective-permute-start = (bf16[512,512]{1,0:T(8,128)(2,1)S(1)}, bf16[512,512]{1,0:T(8,128)(2,1)S(1)}, u32[]{:S(2)}, u32[]{:S(2)}) collective-permute-start(bf16[512,512]{1,0:T(8,128)(2,1)S(1)} %slice.51), channel_id=1, source_target_pairs={{0,1},{1,0},{2,3},{3,2},{4,5},{5,4},{6,7},{7,6},{8,9},{9,8},{10,11... | collective-permute-start | bytes 1572872 | tf_op jit(solution)/shard_map/ppermute | solution.py:46
  20.3 8.9 %collective-permute-start.1 = (bf16[128,512]{1,0:T(8,128)(2,1)S(1)}, bf16[128,512]{1,0:T(8,128)(2,1)S(1)}, u32[]{:S(2)}, u32[]{:S(2)}) collective-permute-start(bf16[128,512]{1,0:T(8,128)(2,1)S(1)} %get-tuple-element.6), channel_id=1, source_target_pairs={{0,2},{1,3},{2,0},{3,1},{4,6},{5,7},{6,4},{7,5},{8,10},{9,11},{10,... | collective-permute-start | bytes 393224 | tf_op jit(solution)/shard_map/ppermute | solution.py:46
  23.3 7.3 %collective-permute-start.3 = (bf16[128,512]{1,0:T(8,128)(2,1)S(1)}, bf16[128,512]{1,0:T(8,128)(2,1)S(1)}, u32[]{:S(2)}, u32[]{:S(2)}) collective-permute-start(bf16[128,512]{1,0:T(8,128)(2,1)S(1)} %get-tuple-element.7), channel_id=1, source_target_pairs={{0,6},{1,7},{2,4},{3,5},{4,2},{5,3},{6,0},{7,1},{8,14},{9,15},{10,... | collective-permute-start | bytes 393224 | tf_op jit(solution)/shard_map/ppermute | solution.py:46
  24.7 6.5 %collective-permute-start.2 = (bf16[128,512]{1,0:T(8,128)(2,1)S(1)}, bf16[128,512]{1,0:T(8,128)(2,1)S(1)}, u32[]{:S(2)}, u32[]{:S(2)}) collective-permute-start(bf16[128,512]{1,0:T(8,128)(2,1)S(1)} %get-tuple-element.8), channel_id=1, source_target_pairs={{0,4},{1,5},{2,6},{3,7},{4,0},{5,1},{6,2},{7,3},{8,12},{9,13},{10,... | collective-permute-start | bytes 393224 | tf_op jit(solution)/shard_map/ppermute | solution.py:46
  31.3 6.1 %collective-permute-start.4 = (bf16[32,512]{1,0:T(8,128)(2,1)S(1)}, bf16[32,512]{1,0:T(8,128)(2,1)S(1)}, u32[]{:S(2)}, u32[]{:S(2)}) collective-permute-start(bf16[32,512]{1,0:T(8,128)(2,1)S(1)} %get-tuple-element.9), channel_id=1, source_target_pairs={{0,8},{1,9},{2,10},{3,11},{4,12},{5,13},{6,14},{7,15},{8,16},{9,17... | collective-permute-start | bytes 98312 | tf_op jit(solution)/shard_map/ppermute | solution.py:46
  33.1 4.3 %collective-permute-start.6 = (bf16[32,512]{1,0:T(8,128)(2,1)S(1)}, bf16[32,512]{1,0:T(8,128)(2,1)S(1)}, u32[]{:S(2)}, u32[]{:S(2)}) collective-permute-start(bf16[32,512]{1,0:T(8,128)(2,1)S(1)} %get-tuple-element.10), channel_id=1, source_target_pairs={{0,24},{1,25},{2,26},{3,27},{4,28},{5,29},{6,30},{7,31},{8,0},{9,1... | collective-permute-start | bytes 98312 | tf_op jit(solution)/shard_map/ppermute | solution.py:46
  35.2 4.8 %collective-permute-start.5 = (bf16[32,512]{1,0:T(8,128)(2,1)S(1)}, bf16[32,512]{1,0:T(8,128)(2,1)S(1)}, u32[]{:S(2)}, u32[]{:S(2)}) collective-permute-start(bf16[32,512]{1,0:T(8,128)(2,1)S(1)} %get-tuple-element.11), channel_id=1, source_target_pairs={{0,16},{1,17},{2,18},{3,19},{4,20},{5,21},{6,22},{7,23},{8,24},{9,... | collective-permute-start | bytes 98312 | tf_op jit(solution)/shard_map/ppermute | solution.py:46

commit v2 on v1

v2 whole, which is shorter than its diff:
```python
import functools

import jax
import jax.numpy as jnp
from jax import lax
from jax.experimental import pallas as pl
from jax.experimental.pallas import tpu as pltpu
from jax.sharding import PartitionSpec as P

HEADS = 8
CORES = 2
LANES = 128

norm_eps = 1e-06
clip_norm = 4.0
learn_rate = 0.5
beta_first = 0.9
beta_second = 0.999
adam_step = 3.0
adam_eps = 1e-08

AXES = ("wide", "narrow")


def layout_of(wide, narrow):
    cores = CORES
    inner = 2 if wide % 2 == 0 else 1
    return cores, inner, narrow // cores, wide // inner


def destination(wide, narrow, w, n, cr, ir, yr, zr):
    cores, inner, pairs, outer = layout_of(wide, narrow)
    z, i = w // inner, w % inner
    y, c = n // cores, n % cores
    w_to = ((z + zr) % outer) * inner + (i + ir) % inner
    n_to = ((y + yr) % pairs) * cores + (c + cr) % cores
    return w_to, n_to


def send(x, wide, narrow, offset):
    perm = []
    for w in range(wide):
        for n in range(narrow):
            w_to, n_to = destination(wide, narrow, w, n, *offset)
            perm.append((w * narrow + n, w_to * narrow + n_to))
    return lax.ppermute(x, AXES, perm)


def dot(a, b):
    return lax.dot_general(a, b, (((1,), (0,)), ((), ())), preferred_element_type=jnp.float32)


def dot_nt(a, b):
    return lax.dot_general(a, b, (((1,), (1,)), ((), ())), preferred_element_type=jnp.float32)


def local_kernel(
    wide, narrow, rows_dev,
    len_hbm, rows_hbm, tok_hbm, cot_hbm, win_hbm, wout_hbm,
    keep_ref, send_ref,
    len_ref, rows_ref, tok, cot, win, wout, hid, slope, att, fac, mixed, inner_grad, dgated, dm_s, dm_t, q_t, dk_t, dv_t, sems,
):
    micro, lmax, width = tok_hbm.shape
    half = lmax // 2
    per_head = width // HEADS
    f32, bf16 = jnp.float32, jnp.bfloat16
    total = micro * lmax
    tile = 256
    tiles = 4 * width // tile

    copies = [pltpu.make_async_copy(tok_hbm, tok, sems.at[0])]
    for t in range(tiles):
        cols = pl.ds(t * tile, tile)
        copies.append(pltpu.make_async_copy(win_hbm.at[:, cols], win.at[:, cols], sems.at[1 + t]))
    copies.append(pltpu.make_async_copy(cot_hbm, cot, sems.at[1 + tiles]))
    copies.append(pltpu.make_async_copy(wout_hbm, wout, sems.at[2 + tiles]))
    copies.append(pltpu.make_async_copy(len_hbm, len_ref, sems.at[3 + tiles]))
    copies.append(pltpu.make_async_copy(rows_hbm, rows_ref, sems.at[4 + tiles]))
    for copy in copies:
        copy.start()

    copies[0].wait()
    source = tok[...].reshape(total, width) * jnp.asarray(0.5, bf16)
    for t in range(tiles):
        cols = pl.ds(t * tile, tile)
        copies[1 + t].wait()
        u = dot(source, win[:, cols])
        th = jnp.tanh(u)
        up = 1.0 + th
        act = u * up
        hid[:, cols] = act.astype(bf16)
        slope[:, cols] = up + act * (1.0 - th)

    row = lax.broadcasted_iota(jnp.int32, (lmax, 1), 0)
    copies[1 + tiles].wait()
    copies[3 + tiles].wait()
    for s in range(micro):
        live = (row < len_ref[s]).astype(f32)
        cot[s] = (cot[s].astype(f32) * live).astype(bf16)
    copies[2 + tiles].wait()
    dgated[...] = dot_nt(cot[...].reshape(total, width), wout[...]).astype(bf16)

    lane = lax.broadcasted_iota(jnp.int32, (1, LANES), 1)
    heads_here = LANES // per_head
    masks = [((lane // per_head) == h).astype(bf16) for h in range(heads_here)]
    scale = per_head ** (-0.5)
    causal = lax.broadcasted_iota(jnp.int32, (half, half), 1) <= lax.broadcasted_iota(jnp.int32, (half, half), 0)
    none = jnp.zeros((half, half), bf16)

    def pick_lanes(stacked):
        out = stacked[:lmax]
        for h in range(1, heads_here):
            out = jnp.where(lane // per_head == h, stacked[h * lmax : (h + 1) * lmax], out)
        return out

    def one_sequence(s, carry):
        base = pl.multiple_of(s * lmax, lmax)
        here = pl.ds(base, lmax)
        length = len_ref[s]
        share = jnp.where(row < length, 1.0 / jnp.full((lmax, 1), length, jnp.int32).astype(f32), 0.0)
        share_half = share * (0.5 * scale)

        for p in range(width // LANES):
            q = hid[here, pl.ds(2 * width + p * LANES, LANES)]
            k = hid[here, pl.ds(3 * width + p * LANES, LANES)]
            v = hid[here, pl.ds(width + p * LANES, LANES)]
            qs = jnp.concatenate([q * (m * jnp.asarray(0.5 * scale, bf16)) for m in masks], axis=0)
            scores = dot_nt(qs, k)
            weights = []
            for h in range(heads_here):
                head = p * heads_here + h
                parts = []
                for b in range(2):
                    rows = slice(b * half, (b + 1) * half)
                    u = scores[h * lmax + b * half : h * lmax + (b + 1) * half, : (b + 1) * half]
                    th = jnp.tanh(u)
                    up = 1.0 + th
                    act = u * up
                    w_b = act * share[rows]
                    f_b = (up + act * (1.0 - th)) * share_half[rows]
                    edge = slice(b * half, (b + 1) * half)
                    diag = jnp.where(causal, w_b[:, edge], 0.0).astype(bf16)
                    fac[head, rows, edge] = jnp.where(causal, f_b[:, edge], 0.0)
                    if b == 0:
                        parts.append(jnp.concatenate([diag, none], axis=1))
                    else:
                        fac[head, rows, :half] = f_b[:, :half]
                        parts.append(jnp.concatenate([w_b[:, :half].astype(bf16), diag], axis=1))
                weight = jnp.concatenate(parts, axis=0)
                att[head] = weight
                weights.append(weight)
            mixed[:, pl.ds(p * LANES, LANES)] = pick_lanes(dot(jnp.concatenate(weights, axis=0), v))

        group = 32
        for r in range(lmax // group):
            rows = pl.ds(r * group, group)
            those = pl.ds(pl.multiple_of(base + r * group, group), group)
            mix = mixed[rows, :]
            centered = mix - jnp.mean(mix, axis=1, keepdims=True)
            inv = lax.rsqrt(jnp.mean(centered * centered, axis=1, keepdims=True) + norm_eps)
            normed = centered * inv
            dg = dgated[those, :].astype(f32)
            gate = hid[those, pl.ds(0, width)].astype(f32)
            dgate = (dg * normed).astype(bf16).astype(f32)
            inner_grad[those, pl.ds(0, width)] = (dgate * slope[those, pl.ds(0, width)]).astype(bf16)
            dn = dg * gate
            dmix = inv * (
                dn - jnp.mean(dn, axis=1, keepdims=True) - normed * jnp.mean(dn * normed, axis=1, keepdims=True)
            )
            dm_s[rows, :] = dmix.astype(bf16)
        dm_t[...] = dm_s[...].T
        q_t[...] = hid[here, pl.ds(2 * width, width)].T

        for p in range(width // LANES):
            k = hid[here, pl.ds(3 * width + p * LANES, LANES)]
            v = hid[here, pl.ds(width + p * LANES, LANES)]
            dmp = dm_s[:, pl.ds(p * LANES, LANES)]
            d_att = dot_nt(jnp.concatenate([dmp * m for m in masks], axis=0), v)
            stacked = []
            for h in range(heads_here):
                head = p * heads_here + h
                d_top = d_att[h * lmax : h * lmax + half, :half].astype(bf16).astype(f32)
                d_low = d_att[h * lmax + half : (h + 1) * lmax].astype(bf16).astype(f32)
                ds_top = (d_top * fac[head, :half, :half]).astype(bf16)
                ds_low = (d_low * fac[head, half:, :]).astype(bf16)
                ds = jnp.concatenate([jnp.concatenate([ds_top, none], axis=1), ds_low], axis=0)
                stacked.append(ds)
                feat = pl.ds(head * per_head, per_head)
                dk_t[feat, :] = dot(q_t[feat, :], ds).astype(bf16)
                dv_t[feat, :] = dot(dm_t[feat, :], att[head]).astype(bf16)
            dq = pick_lanes(dot(jnp.concatenate(stacked, axis=0), k)).astype(bf16).astype(f32)
            cols = pl.ds(2 * width + p * LANES, LANES)
            inner_grad[here, cols] = (dq * slope[here, cols]).astype(bf16)
        for part, source_t in ((1, dv_t), (3, dk_t)):
            cols = pl.ds(part * width, width)
            inner_grad[here, cols] = (source_t[...].T.astype(f32) * slope[here, cols]).astype(bf16)
        return carry

    lax.fori_loop(0, micro, one_sequence, 0)

    back = (0.5 * dot_nt(inner_grad[...], win[...])).astype(bf16).astype(f32)
    grads = (back + cot[...].reshape(total, width).astype(f32)).astype(bf16)
    dgated[...] = grads

    copies[4 + tiles].wait()
    cores, inner_w, pairs, outer = layout_of(wide, narrow)
    w_me, n_me = lax.axis_index("wide"), lax.axis_index("narrow")
    z_me, i_me = w_me // inner_w, w_me % inner_w
    y_me, c_me = n_me // cores, n_me % cores
    blocks = wide * narrow // cores
    per_chunk = min(8, blocks)
    size = per_chunk * rows_dev
    slot = lax.broadcasted_iota(jnp.int32, (rows_dev, lmax), 0)

    def fill(out_ref, core_offset):
        def one_chunk(j, carry):
            pieces = []
            for b in range(per_chunk):
                block = j * per_chunk + b
                zr = block % outer
                yr = (block // outer) % pairs
                ir = block // (outer * pairs)
                w_to = ((z_me + zr) % outer) * inner_w + (i_me + ir) % inner_w
                n_to = ((y_me + yr) % pairs) * cores + (c_me + core_offset) % cores
                want = slot + (w_to * narrow + n_to) * rows_dev
                pieces.append(
                    jnp.concatenate(
                        [(want == rows_ref[s : s + 1, :]).astype(f32).astype(bf16) for s in range(micro)], axis=1
                    )
                )
            chosen = jnp.concatenate(pieces, axis=0)
            out_ref[pl.ds(pl.multiple_of(j * size, size), size), :] = dot(chosen, dgated[...]).astype(bf16)
            return carry

        lax.fori_loop(0, blocks // per_chunk, one_chunk, 0, unroll=blocks // per_chunk <= 4)

    fill(send_ref, 1)
    fill(keep_ref, 0)


def local_rows(wide, narrow, rows_dev, tokens, cotangent, lengths, item_rows, w_in, w_out):
    micro, lmax, width = tokens.shape
    total = micro * lmax
    items = wide * narrow * rows_dev
    f32, bf16 = jnp.float32, jnp.bfloat16
    vmem = pl.BlockSpec(memory_space=pltpu.VMEM)
    hbm = pl.BlockSpec(memory_space=pltpu.HBM)
    part = jax.ShapeDtypeStruct((items // CORES, width), bf16)
    tiles = 4 * width // 256
    return pl.pallas_call(
        functools.partial(local_kernel, wide, narrow, rows_dev),
        out_shape=(part, part),
        in_specs=[hbm] * 6,
        out_specs=(vmem, vmem),
        scratch_shapes=[
            pltpu.SMEM((micro,), jnp.int32),
            pltpu.VMEM((micro, lmax), jnp.int32),
            pltpu.VMEM((micro, lmax, width), bf16),
            pltpu.VMEM((micro, lmax, width), bf16),
            pltpu.VMEM((width, 4 * width), bf16),
            pltpu.VMEM((width, width), bf16),
            pltpu.VMEM((total, 4 * width), bf16),
            pltpu.VMEM((total, 4 * width), f32),
            pltpu.VMEM((HEADS, lmax, lmax), bf16),
            pltpu.VMEM((HEADS, lmax, lmax), f32),
            pltpu.VMEM((lmax, width), f32),
            pltpu.VMEM((total, 4 * width), bf16),
            pltpu.VMEM((total, width), bf16),
            pltpu.VMEM((lmax, width), bf16),
            pltpu.VMEM((width, lmax), bf16),
            pltpu.VMEM((width, lmax), bf16),
            pltpu.VMEM((width, lmax), bf16),
            pltpu.VMEM((width, lmax), bf16),
            pltpu.SemaphoreType.DMA((tiles + 5,)),
        ],
        compiler_params=pltpu.CompilerParams(vmem_limit_bytes=(28 << 20) + 4 * items * width),
        cost_estimate=pl.CostEstimate(
            flops=16 * total * width * width + 12 * total * lmax * width,
            bytes_accessed=4 * total * width + 10 * width * width + 2 * items * width,
            transcendentals=HEADS * total * lmax,
        ),
        name="local_rows",
    )(*(pltpu.with_memory_space_constraint(a, pltpu.HBM) for a in (lengths, item_rows, tokens, cotangent, w_in, w_out)))


def adam_rows(row_grad, table, moment_one, moment_two):
    row_norms = jnp.sqrt(jnp.sum(row_grad * row_grad, axis=1, keepdims=True))
    clipped = row_grad * (clip_norm / jnp.maximum(row_norms, clip_norm))
    first_moment = beta_first * moment_one + (1.0 - beta_first) * clipped
    second_moment = beta_second * moment_two + (1.0 - beta_second) * clipped * clipped
    step_size = learn_rate / (1.0 - beta_first**adam_step)
    scaled = jnp.sqrt(second_moment / (1.0 - beta_second**adam_step)) + adam_eps
    return (table - step_size * first_moment / scaled, first_moment, second_moment)


def gather_sum(pieces, offsets, wide, narrow):
    arrived = [send(pieces[k], wide, narrow, offsets[k]) for k in range(1, len(offsets))]
    out = pieces[0].astype(jnp.float32)
    for piece in arrived:
        out = out + piece.astype(jnp.float32)
    return out


def on_device(tokens, cotangent, lengths, item_rows, w_in, w_out, table, moment_one, moment_two):
    wide, narrow = lax.axis_size("wide"), lax.axis_size("narrow")
    rows_dev, width = table.shape
    cores, inner, pairs, outer = layout_of(wide, narrow)
    held = local_rows(wide, narrow, rows_dev, tokens, cotangent, lengths, item_rows, w_in, w_out)
    stages = (
        [(c, 0, 0, 0) for c in range(cores)],
        [(0, i, y, 0) for i in range(inner) for y in range(pairs)],
        [(0, 0, 0, z) for z in range(outer)],
    )
    for number, offsets in enumerate(stages):
        if number:
            held = held.astype(jnp.bfloat16).reshape(len(offsets), -1, width)
        held = gather_sum(held, offsets, wide, narrow)
    return adam_rows(held, table, moment_one, moment_two)


def solution(mesh):
    return jax.shard_map(
        on_device,
        mesh=mesh,
        in_specs=(
            P(AXES, None, None),
            P(AXES, None, None),
            P(AXES),
            P(AXES, None),
            P(),
            P(),
            P(AXES, None),
            P(AXES, None),
            P(AXES, None),
        ),
        out_specs=(P(AXES, None), P(AXES, None), P(AXES, None)),
        check_vma=False,
    )
```

time: 41.1 us -> 36.2 us (0.88)
  Pallas kernels: 15.3 us -> 12.5 us
  local copies, waits for them, and re-layouts: 1.16 us -> 0.06 us
  other arithmetic: 2.16 us -> 1.12 us
    pallas_call x1, Pallas kernels: 15.3 us -> 12.5 us  [local_rows(): pl.pallas_call(functools.partial(local_kernel, wide, narrow, rows_dev), o...]
    slice x3 -> x2, local copies, waits for them, and re-layouts: 1.15 us -> 0.04 us  [gather_sum(): pieces[k]]
    convert_element_type x2, other arithmetic: 1.24 us -> 0.2 us  [on_device(): held = held.astype(jnp.bfloat16).reshape(len(offsets), -1, width)]
where the time goes in v2:
time: 36.2 us; the launch traced here: 36 us
  Pallas kernels  12.5 us (35%)
  waiting for transfers between devices  11.8 us (33%)
  starting transfers between devices  9.85 us (27%)
  other arithmetic  1.12 us (3%)
  between operations  0.71 us (2%)
    pallas_call x1, Pallas kernels, local_rows(): pl.pallas_call(functools.partial(local_kernel, wide, narrow, rows_dev), o...  12.5 us
    ppermute x7, waiting for transfers between devices, send(): return lax.ppermute(x, AXES, perm)  11.8 us
    ppermute x7, starting transfers between devices, send(): return lax.ppermute(x, AXES, perm)  9.85 us
    sub x1, other arithmetic, adam_rows(): table - step_size * first_moment / scaled  0.78 us
  transfers between devices with their start and end apart: 7, of which 6 were waited for; matrix products, arithmetic and copies ran while one was open for 0% of the time, Pallas kernels for 0%

profile of v2, /device:TPU:0, one launch (start us, length us, event | category | flops | bytes accessed | tf_op | source)
XLA Modules:
  0.0 36.0 jit_solution(12392470323501047462)
XLA Ops:
  0.6 12.5 %local_rows.1 = (bf16[512,512]{1,0:T(8,128)(2,1)S(1)}, bf16[512,512]{1,0:T(8,128)(2,1)S(1)}) custom-call(s32[2]{0:T(128)} %len_hbm.1, s32[2,256]{1,0:T(2,128)} %rows_hbm.1, bf16[2,256,512]{2,1,0:T(8,128)(2,1)} %tok_hbm.1, bf16[2,256,512]{2,1,0:T(8,128)(2,1)} %cot_hbm.1, bf16[512,2048]{1,0:T(8,128)(2,1)} %win_hbm.1, bf16[512,512]{1,0:T(8,128)(2,1)} %wout_hbm.1), custom_call_target="tpu_custom_call" | custom-call | flops 2952790016 | bytes 4718592 | tf_op jit(solution)/shard_map/local_rows/pallas_call | solution.py:250
  13.2 0.0 copy-start
  13.2 0.0 copy-start.1
  13.2 0.0 copy-start.2
  13.2 0.6 %collective-permute-start = (bf16[512,512]{1,0:T(8,128)(2,1)S(1)}, bf16[512,512]{1,0:T(8,128)(2,1)S(1)}, u32[]{:S(2)}, u32[]{:S(2)}) collective-permute-start(bf16[512,512]{1,0:T(8,128)(2,1)S(1)} %get-tuple-element.6), channel_id=1, source_target_pairs={{0,1},{1,0},{2,3},{3,2},{4,5},{5,4},{6,7},{7,6},{8,9},{9,8},{10,11... | collective-permute-start | bytes 1572872 | tf_op jit(solution)/shard_map/ppermute | solution.py:46
  13.8 1.5 %collective-permute-done = bf16[512,512]{1,0:T(8,128)(2,1)S(1)} collective-permute-done((bf16[512,512]{1,0:T(8,128)(2,1)S(1)}, bf16[512,512]{1,0:T(8,128)(2,1)S(1)}, u32[]{:S(2)}, u32[]{:S(2)}) %collective-permute-start) | collective-permute-done | bytes 524320 | tf_op jit(solution)/shard_map/ppermute | solution.py:46
  15.3 0.1 add_convert_fusion
  15.5 2.9 %collective-permute-start.1 = (bf16[128,512]{1,0:T(8,128)(2,1)S(1)}, bf16[128,512]{1,0:T(8,128)(2,1)S(1)}, u32[]{:S(2)}, u32[]{:S(2)}) collective-permute-start(bf16[128,512]{1,0:T(8,128)(2,1)S(1)} %get-tuple-element.10), channel_id=1, source_target_pairs={{0,2},{1,3},{2,0},{3,1},{4,6},{5,7},{6,4},{7,5},{8,10},{9,11},{10,... | collective-permute-start | bytes 393224 | tf_op jit(solution)/shard_map/ppermute | solution.py:46
  18.4 1.4 %collective-permute-start.3 = (bf16[128,512]{1,0:T(8,128)(2,1)S(1)}, bf16[128,512]{1,0:T(8,128)(2,1)S(1)}, u32[]{:S(2)}, u32[]{:S(2)}) collective-permute-start(bf16[128,512]{1,0:T(8,128)(2,1)S(1)} %get-tuple-element.11), channel_id=1, source_target_pairs={{0,6},{1,7},{2,4},{3,5},{4,2},{5,3},{6,0},{7,1},{8,14},{9,15},{10,... | collective-permute-start | bytes 393224 | tf_op jit(solution)/shard_map/ppermute | solution.py:46
  19.8 0.1 collective-permute-start.2
  19.9 4.4 %collective-permute-done.1 = bf16[128,512]{1,0:T(8,128)(2,1)S(1)} collective-permute-done((bf16[128,512]{1,0:T(8,128)(2,1)S(1)}, bf16[128,512]{1,0:T(8,128)(2,1)S(1)}, u32[]{:S(2)}, u32[]{:S(2)}) %collective-permute-start.1) | collective-permute-done | bytes 131104 | tf_op jit(solution)/shard_map/ppermute | solution.py:46
  24.3 1.3 %collective-permute-done.3 = bf16[128,512]{1,0:T(8,128)(2,1)S(1)} collective-permute-done((bf16[128,512]{1,0:T(8,128)(2,1)S(1)}, bf16[128,512]{1,0:T(8,128)(2,1)S(1)}, u32[]{:S(2)}, u32[]{:S(2)}) %collective-permute-start.3) | collective-permute-done | bytes 131104 | tf_op jit(solution)/shard_map/ppermute | solution.py:46
  25.7 0.6 %collective-permute-done.2 = bf16[128,512]{1,0:T(8,128)(2,1)S(1)} collective-permute-done((bf16[128,512]{1,0:T(8,128)(2,1)S(1)}, bf16[128,512]{1,0:T(8,128)(2,1)S(1)}, u32[]{:S(2)}, u32[]{:S(2)}) %collective-permute-start.2) | collective-permute-done | bytes 131104 | tf_op jit(solution)/shard_map/ppermute | solution.py:46
  26.3 0.1 add_convert_fusion.1
  26.4 1.8 %collective-permute-start.4 = (bf16[32,512]{1,0:T(8,128)(2,1)S(1)}, bf16[32,512]{1,0:T(8,128)(2,1)S(1)}, u32[]{:S(2)}, u32[]{:S(2)}) collective-permute-start(bf16[32,512]{1,0:T(8,128)(2,1)S(1)} %get-tuple-element.13), channel_id=1, source_target_pairs={{0,8},{1,9},{2,10},{3,11},{4,12},{5,13},{6,14},{7,15},{8,16},{9,17... | collective-permute-start | bytes 98312 | tf_op jit(solution)/shard_map/ppermute | solution.py:46
  28.2 2.1 %collective-permute-start.6 = (bf16[32,512]{1,0:T(8,128)(2,1)S(1)}, bf16[32,512]{1,0:T(8,128)(2,1)S(1)}, u32[]{:S(2)}, u32[]{:S(2)}) collective-permute-start(bf16[32,512]{1,0:T(8,128)(2,1)S(1)} %get-tuple-element.14), channel_id=1, source_target_pairs={{0,24},{1,25},{2,26},{3,27},{4,28},{5,29},{6,30},{7,31},{8,0},{9,1... | collective-permute-start | bytes 98312 | tf_op jit(solution)/shard_map/ppermute | solution.py:46
  30.3 0.9 %collective-permute-start.5 = (bf16[32,512]{1,0:T(8,128)(2,1)S(1)}, bf16[32,512]{1,0:T(8,128)(2,1)S(1)}, u32[]{:S(2)}, u32[]{:S(2)}) collective-permute-start(bf16[32,512]{1,0:T(8,128)(2,1)S(1)} %get-tuple-element.15), channel_id=1, source_target_pairs={{0,16},{1,17},{2,18},{3,19},{4,20},{5,21},{6,22},{7,23},{8,24},{9,... | collective-permute-start | bytes 98312 | tf_op jit(solution)/shard_map/ppermute | solution.py:46
  31.2 1.3 %collective-permute-done.4 = bf16[32,512]{1,0:T(8,128)(2,1)S(1)} collective-permute-done((bf16[32,512]{1,0:T(8,128)(2,1)S(1)}, bf16[32,512]{1,0:T(8,128)(2,1)S(1)}, u32[]{:S(2)}, u32[]{:S(2)}) %collective-permute-start.4) | collective-permute-done | bytes 32800 | tf_op jit(solution)/shard_map/ppermute | solution.py:46
  32.5 0.0 collective-permute-done.6
  32.5 2.6 %collective-permute-done.5 = bf16[32,512]{1,0:T(8,128)(2,1)S(1)} collective-permute-done((bf16[32,512]{1,0:T(8,128)(2,1)S(1)}, bf16[32,512]{1,0:T(8,128)(2,1)S(1)}, u32[]{:S(2)}, u32[]{:S(2)}) %collective-permute-start.5) | collective-permute-done | bytes 32800 | tf_op jit(solution)/shard_map/ppermute | solution.py:46
  35.1 0.1 multiply_reduce_fusion
  35.2 0.0 copy-done
  35.2 0.0 copy-done.1
  35.2 0.0 copy-done.2
  35.3 0.8 %divide_subtract_fusion = (f32[32,512]{1,0:T(8,128)}, f32[32,512]{1,0:T(8,128)}, f32[32,512]{1,0:T(8,128)}) fusion(f32[32,512]{1,0:T(8,128)S(1)} %copy-done, f32[32]{0:T(128)S(1)} %maximum_divide_fusion, bf16[32,512]{1,0:T(8,128)(2,1)S(1)} %collective-permute-done.6, bf16[32,512]{1,0:T(8,128)(2,1)S(1)} %collective-permute-done.5, ...), kind=kLoop, calls=%fused_computation.4 | loop fusion | flops 327680 | bytes 524416 | tf_op jit(solution)/shard_map/sub | solution.py:293
  (3 shorter events, 0.0 us)
Async XLA Ops:
  13.2 22.1 %copy-start = (f32[32,512]{1,0:T(8,128)S(1)}, f32[32,512]{1,0:T(8,128)}, u32[]{:S(2)}) copy-start(f32[32,512]{1,0:T(8,128)} %param.15) | copy-start | bytes 196612
  13.2 22.1 %copy-start.1 = (f32[32,512]{1,0:T(8,128)S(1)}, f32[32,512]{1,0:T(8,128)}, u32[]{:S(2)}) copy-start(f32[32,512]{1,0:T(8,128)} %param.16) | copy-start | bytes 196612
  13.2 22.1 %copy-start.2 = (f32[32,512]{1,0:T(8,128)S(1)}, f32[32,512]{1,0:T(8,128)}, u32[]{:S(2)}) copy-start(f32[32,512]{1,0:T(8,128)} %param.17) | copy-start | bytes 196612
  13.2 2.1 %collective-permute-start = (bf16[512,512]{1,0:T(8,128)(2,1)S(1)}, bf16[512,512]{1,0:T(8,128)(2,1)S(1)}, u32[]{:S(2)}, u32[]{:S(2)}) collective-permute-start(bf16[512,512]{1,0:T(8,128)(2,1)S(1)} %get-tuple-element.6), channel_id=1, source_target_pairs={{0,1},{1,0},{2,3},{3,2},{4,5},{5,4},{6,7},{7,6},{8,9},{9,8},{10,11... | collective-permute-start | bytes 1572872 | tf_op jit(solution)/shard_map/ppermute | solution.py:46
  15.5 8.9 %collective-permute-start.1 = (bf16[128,512]{1,0:T(8,128)(2,1)S(1)}, bf16[128,512]{1,0:T(8,128)(2,1)S(1)}, u32[]{:S(2)}, u32[]{:S(2)}) collective-permute-start(bf16[128,512]{1,0:T(8,128)(2,1)S(1)} %get-tuple-element.10), channel_id=1, source_target_pairs={{0,2},{1,3},{2,0},{3,1},{4,6},{5,7},{6,4},{7,5},{8,10},{9,11},{10,... | collective-permute-start | bytes 393224 | tf_op jit(solution)/shard_map/ppermute | solution.py:46
  18.4 7.3 %collective-permute-start.3 = (bf16[128,512]{1,0:T(8,128)(2,1)S(1)}, bf16[128,512]{1,0:T(8,128)(2,1)S(1)}, u32[]{:S(2)}, u32[]{:S(2)}) collective-permute-start(bf16[128,512]{1,0:T(8,128)(2,1)S(1)} %get-tuple-element.11), channel_id=1, source_target_pairs={{0,6},{1,7},{2,4},{3,5},{4,2},{5,3},{6,0},{7,1},{8,14},{9,15},{10,... | collective-permute-start | bytes 393224 | tf_op jit(solution)/shard_map/ppermute | solution.py:46
  19.8 6.5 %collective-permute-start.2 = (bf16[128,512]{1,0:T(8,128)(2,1)S(1)}, bf16[128,512]{1,0:T(8,128)(2,1)S(1)}, u32[]{:S(2)}, u32[]{:S(2)}) collective-permute-start(bf16[128,512]{1,0:T(8,128)(2,1)S(1)} %get-tuple-element.12), channel_id=1, source_target_pairs={{0,4},{1,5},{2,6},{3,7},{4,0},{5,1},{6,2},{7,3},{8,12},{9,13},{10,... | collective-permute-start | bytes 393224 | tf_op jit(solution)/shard_map/ppermute | solution.py:46
  26.4 6.1 %collective-permute-start.4 = (bf16[32,512]{1,0:T(8,128)(2,1)S(1)}, bf16[32,512]{1,0:T(8,128)(2,1)S(1)}, u32[]{:S(2)}, u32[]{:S(2)}) collective-permute-start(bf16[32,512]{1,0:T(8,128)(2,1)S(1)} %get-tuple-element.13), channel_id=1, source_target_pairs={{0,8},{1,9},{2,10},{3,11},{4,12},{5,13},{6,14},{7,15},{8,16},{9,17... | collective-permute-start | bytes 98312 | tf_op jit(solution)/shard_map/ppermute | solution.py:46
  28.2 4.3 %collective-permute-start.6 = (bf16[32,512]{1,0:T(8,128)(2,1)S(1)}, bf16[32,512]{1,0:T(8,128)(2,1)S(1)}, u32[]{:S(2)}, u32[]{:S(2)}) collective-permute-start(bf16[32,512]{1,0:T(8,128)(2,1)S(1)} %get-tuple-element.14), channel_id=1, source_target_pairs={{0,24},{1,25},{2,26},{3,27},{4,28},{5,29},{6,30},{7,31},{8,0},{9,1... | collective-permute-start | bytes 98312 | tf_op jit(solution)/shard_map/ppermute | solution.py:46
  30.3 4.8 %collective-permute-start.5 = (bf16[32,512]{1,0:T(8,128)(2,1)S(1)}, bf16[32,512]{1,0:T(8,128)(2,1)S(1)}, u32[]{:S(2)}, u32[]{:S(2)}) collective-permute-start(bf16[32,512]{1,0:T(8,128)(2,1)S(1)} %get-tuple-element.15), channel_id=1, source_target_pairs={{0,16},{1,17},{2,18},{3,19},{4,20},{5,21},{6,22},{7,23},{8,24},{9,... | collective-permute-start | bytes 98312 | tf_op jit(solution)/shard_map/ppermute | solution.py:46

commit v3 on v2

v3 whole, which is shorter than its diff:
```python
import functools

import jax
import jax.numpy as jnp
from jax import lax
from jax.experimental import pallas as pl
from jax.experimental.pallas import tpu as pltpu
from jax.sharding import PartitionSpec as P

HEADS = 8
CORES = 2
LANES = 128

norm_eps = 1e-06
clip_norm = 4.0
learn_rate = 0.5
beta_first = 0.9
beta_second = 0.999
adam_step = 3.0
adam_eps = 1e-08

AXES = ("wide", "narrow")


def layout_of(wide, narrow):
    cores = CORES
    inner = 2 if wide % 2 == 0 else 1
    return cores, inner, narrow // cores, wide // inner


def destination(wide, narrow, w, n, cr, ir, yr, zr):
    cores, inner, pairs, outer = layout_of(wide, narrow)
    z, i = w // inner, w % inner
    y, c = n // cores, n % cores
    w_to = ((z + zr) % outer) * inner + (i + ir) % inner
    n_to = ((y + yr) % pairs) * cores + (c + cr) % cores
    return w_to, n_to


def send(x, wide, narrow, offset):
    perm = []
    for w in range(wide):
        for n in range(narrow):
            w_to, n_to = destination(wide, narrow, w, n, *offset)
            perm.append((w * narrow + n, w_to * narrow + n_to))
    return lax.ppermute(x, AXES, perm)


def dot(a, b):
    return lax.dot_general(a, b, (((1,), (0,)), ((), ())), preferred_element_type=jnp.float32)


def dot_nt(a, b):
    return lax.dot_general(a, b, (((1,), (1,)), ((), ())), preferred_element_type=jnp.float32)


def local_kernel(
    wide, narrow, rows_dev,
    len_hbm, rows_hbm, tok_hbm, cot_hbm, win_hbm, wout_hbm,
    keep_ref, send_ref,
    len_ref, rows_ref, tok, cot, win, wout, hid, slope, att, fac, mixed, inner_grad, dgated, dm_s, sems,
):
    micro, lmax, width = tok_hbm.shape
    half = lmax // 2
    per_head = width // HEADS
    f32, bf16 = jnp.float32, jnp.bfloat16
    total = micro * lmax
    bounds = (0, width, 2 * width, 4 * width)
    moves = [(tok_hbm, tok)]
    moves += [(win_hbm.at[:, lo:hi], win.at[:, lo:hi]) for lo, hi in zip(bounds, bounds[1:])]
    moves += [(wout_hbm, wout), (cot_hbm, cot), (len_hbm, len_ref), (rows_hbm, rows_ref)]
    copies = [pltpu.make_async_copy(src, dst, sems.at[i]) for i, (src, dst) in enumerate(moves)]
    for copy in copies:
        copy.start()

    tile = 256
    row = lax.broadcasted_iota(jnp.int32, (lmax, 1), 0)
    copies[0].wait()
    source = tok[...].reshape(total, width) * jnp.asarray(0.5, bf16)
    for part, (lo, hi) in enumerate(zip(bounds, bounds[1:])):
        copies[1 + part].wait()
        if hi == 4 * width:
            for copy in copies[len(bounds) :]:
                copy.wait()
            for s in range(micro):
                live = (row < len_ref[s]).astype(f32)
                cot[s] = (cot[s].astype(f32) * live).astype(bf16)
        for first in range(lo, hi, tile):
            cols = pl.ds(first, tile)
            u = dot(source, win[:, cols])
            th = jnp.tanh(u)
            up = 1.0 + th
            act = u * up
            hid[:, cols] = act.astype(bf16)
            slope[:, cols] = up + act * (1.0 - th)
    dgated[...] = dot_nt(cot[...].reshape(total, width), wout[...]).astype(bf16)

    lane = lax.broadcasted_iota(jnp.int32, (1, LANES), 1)
    heads_here = LANES // per_head
    masks = [((lane // per_head) == h).astype(bf16) for h in range(heads_here)]
    scale = per_head ** (-0.5)
    causal = lax.broadcasted_iota(jnp.int32, (half, half), 1) <= lax.broadcasted_iota(jnp.int32, (half, half), 0)
    none = jnp.zeros((half, half), bf16)
    lane_pairs = width // LANES
    group = 32
    groups = lmax // group

    def pick_lanes(stacked):
        out = stacked[:lmax]
        for h in range(1, heads_here):
            out = jnp.where(lane // per_head == h, stacked[h * lmax : (h + 1) * lmax], out)
        return out

    def forward_pair(s, p):
        here = pl.ds(s * lmax, lmax)
        length = len_ref[s]
        share = jnp.where(row < length, 1.0 / jnp.full((lmax, 1), length, jnp.int32).astype(f32), 0.0)
        share_half = share * (0.5 * scale)
        q = hid[here, pl.ds(2 * width + p * LANES, LANES)]
        k = hid[here, pl.ds(3 * width + p * LANES, LANES)]
        v = hid[here, pl.ds(width + p * LANES, LANES)]
        qs = jnp.concatenate([q * (m * jnp.asarray(0.5 * scale, bf16)) for m in masks], axis=0)
        scores = dot_nt(qs, k)
        weights = []
        for h in range(heads_here):
            head = p * heads_here + h
            parts = []
            for b in range(2):
                rows = slice(b * half, (b + 1) * half)
                u = scores[h * lmax + b * half : h * lmax + (b + 1) * half, : (b + 1) * half]
                th = jnp.tanh(u)
                up = 1.0 + th
                act = u * up
                w_b = act * share[rows]
                f_b = (up + act * (1.0 - th)) * share_half[rows]
                diag = jnp.where(causal, w_b[:, rows], 0.0).astype(bf16)
                fac[s, head, rows, rows] = jnp.where(causal, f_b[:, rows], 0.0)
                if b == 0:
                    parts.append(jnp.concatenate([diag, none], axis=1))
                else:
                    fac[s, head, rows, :half] = f_b[:, :half]
                    parts.append(jnp.concatenate([w_b[:, :half].astype(bf16), diag], axis=1))
            weight = jnp.concatenate(parts, axis=0)
            att[s, head] = weight
            weights.append(weight)
        mixed[s, :, pl.ds(p * LANES, LANES)] = pick_lanes(dot(jnp.concatenate(weights, axis=0), v))

    def norm_group(s, r):
        rows = pl.ds(r * group, group)
        those = pl.ds(s * lmax + r * group, group)
        mix = mixed[s, rows, :]
        centered = mix - jnp.mean(mix, axis=1, keepdims=True)
        inv = lax.rsqrt(jnp.mean(centered * centered, axis=1, keepdims=True) + norm_eps)
        normed = centered * inv
        dg = dgated[those, :].astype(f32)
        gate = hid[those, pl.ds(0, width)].astype(f32)
        dgate = (dg * normed).astype(bf16).astype(f32)
        inner_grad[those, pl.ds(0, width)] = (dgate * slope[those, pl.ds(0, width)]).astype(bf16)
        dn = dg * gate
        dmix = inv * (
            dn - jnp.mean(dn, axis=1, keepdims=True) - normed * jnp.mean(dn * normed, axis=1, keepdims=True)
        )
        dm_s[s, rows, :] = dmix.astype(bf16)

    def backward_pair(s, p):
        here = pl.ds(s * lmax, lmax)
        lanes = pl.ds(p * LANES, LANES)
        q_t = hid[here, pl.ds(2 * width + p * LANES, LANES)].T
        k = hid[here, pl.ds(3 * width + p * LANES, LANES)]
        v = hid[here, pl.ds(width + p * LANES, LANES)]
        dmp = dm_s[s, :, lanes]
        dm_t = dmp.T
        d_att = dot_nt(jnp.concatenate([dmp * m for m in masks], axis=0), v)
        stacked, dks, dvs = [], [], []
        for h in range(heads_here):
            head = p * heads_here + h
            feat = slice(h * per_head, (h + 1) * per_head)
            dvs.append(dot(dm_t[feat], att[s, head]).astype(bf16))
            d_top = d_att[h * lmax : h * lmax + half, :half].astype(bf16).astype(f32)
            d_low = d_att[h * lmax + half : (h + 1) * lmax].astype(bf16).astype(f32)
            ds_top = (d_top * fac[s, head, :half, :half]).astype(bf16)
            ds_low = (d_low * fac[s, head, half:, :]).astype(bf16)
            ds = jnp.concatenate([jnp.concatenate([ds_top, none], axis=1), ds_low], axis=0)
            stacked.append(ds)
            dks.append(dot(q_t[feat], ds).astype(bf16))
        dv = jnp.concatenate(dvs, axis=0).T.astype(f32)
        dk = jnp.concatenate(dks, axis=0).T.astype(f32)
        dq = pick_lanes(dot(jnp.concatenate(stacked, axis=0), k)).astype(bf16).astype(f32)
        for part, piece in ((1, dv), (2, dq), (3, dk)):
            cols = pl.ds(part * width + p * LANES, LANES)
            inner_grad[here, cols] = (piece * slope[here, cols]).astype(bf16)

    each = -(-groups // lane_pairs)
    norm_chunks = [range(p * each, min((p + 1) * each, groups)) for p in range(lane_pairs)]
    for s in range(micro):
        for p in range(lane_pairs):
            forward_pair(s, p)
            if s > 0:
                for r in norm_chunks[p]:
                    norm_group(s - 1, r)
        if s > 0:
            for p in range(lane_pairs):
                backward_pair(s - 1, p)
                if s == micro - 1:
                    for r in norm_chunks[p]:
                        norm_group(s, r)
    if micro == 1:
        for r in range(groups):
            norm_group(0, r)
    for p in range(lane_pairs):
        backward_pair(micro - 1, p)

    back = (0.5 * dot_nt(inner_grad[...], win[...])).astype(bf16).astype(f32)
    grads = (back + cot[...].reshape(total, width).astype(f32)).astype(bf16)
    dgated[...] = grads

    cores, inner_w, pairs, outer = layout_of(wide, narrow)
    w_me, n_me = lax.axis_index("wide"), lax.axis_index("narrow")
    z_me, i_me = w_me // inner_w, w_me % inner_w
    y_me, c_me = n_me // cores, n_me % cores
    blocks = wide * narrow // cores
    per_chunk = min(8, blocks)
    size = per_chunk * rows_dev
    slot = lax.broadcasted_iota(jnp.int32, (rows_dev, lmax), 0)

    def fill(out_ref, core_offset):
        def one_chunk(j, carry):
            pieces = []
            for b in range(per_chunk):
                block = j * per_chunk + b
                zr = block % outer
                yr = (block // outer) % pairs
                ir = block // (outer * pairs)
                w_to = ((z_me + zr) % outer) * inner_w + (i_me + ir) % inner_w
                n_to = ((y_me + yr) % pairs) * cores + (c_me + core_offset) % cores
                want = slot + (w_to * narrow + n_to) * rows_dev
                pieces.append(
                    jnp.concatenate(
                        [(want == rows_ref[s : s + 1, :]).astype(f32).astype(bf16) for s in range(micro)], axis=1
                    )
                )
            chosen = jnp.concatenate(pieces, axis=0)
            out_ref[pl.ds(pl.multiple_of(j * size, size), size), :] = dot(chosen, dgated[...]).astype(bf16)
            return carry

        lax.fori_loop(0, blocks // per_chunk, one_chunk, 0, unroll=blocks // per_chunk <= 4)

    fill(send_ref, 1)
    fill(keep_ref, 0)


def local_rows(wide, narrow, rows_dev, tokens, cotangent, lengths, item_rows, w_in, w_out):
    micro, lmax, width = tokens.shape
    total = micro * lmax
    items = wide * narrow * rows_dev
    f32, bf16 = jnp.float32, jnp.bfloat16
    vmem = pl.BlockSpec(memory_space=pltpu.VMEM)
    hbm = pl.BlockSpec(memory_space=pltpu.HBM)
    part = jax.ShapeDtypeStruct((items // CORES, width), bf16)
    return pl.pallas_call(
        functools.partial(local_kernel, wide, narrow, rows_dev),
        out_shape=(part, part),
        in_specs=[hbm] * 6,
        out_specs=(vmem, vmem),
        scratch_shapes=[
            pltpu.SMEM((micro,), jnp.int32),
            pltpu.VMEM((micro, lmax), jnp.int32),
            pltpu.VMEM((micro, lmax, width), bf16),
            pltpu.VMEM((micro, lmax, width), bf16),
            pltpu.VMEM((width, 4 * width), bf16),
            pltpu.VMEM((width, width), bf16),
            pltpu.VMEM((total, 4 * width), bf16),
            pltpu.VMEM((total, 4 * width), f32),
            pltpu.VMEM((micro, HEADS, lmax, lmax), bf16),
            pltpu.VMEM((micro, HEADS, lmax, lmax), f32),
            pltpu.VMEM((micro, lmax, width), f32),
            pltpu.VMEM((total, 4 * width), bf16),
            pltpu.VMEM((total, width), bf16),
            pltpu.VMEM((micro, lmax, width), bf16),
            pltpu.SemaphoreType.DMA((8,)),
        ],
        compiler_params=pltpu.CompilerParams(vmem_limit_bytes=(28 << 20) + 4 * items * width),
        cost_estimate=pl.CostEstimate(
            flops=16 * total * width * width + 12 * total * lmax * width,
            bytes_accessed=4 * total * width + 10 * width * width + 2 * items * width,
            transcendentals=HEADS * total * lmax,
        ),
        name="local_rows",
    )(*(pltpu.with_memory_space_constraint(a, pltpu.HBM) for a in (lengths, item_rows, tokens, cotangent, w_in, w_out)))


def adam_rows(row_grad, table, moment_one, moment_two):
    row_norms = jnp.sqrt(jnp.sum(row_grad * row_grad, axis=1, keepdims=True))
    clipped = row_grad * (clip_norm / jnp.maximum(row_norms, clip_norm))
    first_moment = beta_first * moment_one + (1.0 - beta_first) * clipped
    second_moment = beta_second * moment_two + (1.0 - beta_second) * clipped * clipped
    step_size = learn_rate / (1.0 - beta_first**adam_step)
    scaled = jnp.sqrt(second_moment / (1.0 - beta_second**adam_step)) + adam_eps
    return (table - step_size * first_moment / scaled, first_moment, second_moment)


def gather_sum(pieces, offsets, order, wide, narrow):
    arrived = [send(pieces[k], wide, narrow, offsets[k]) for k in order]
    out = pieces[0].astype(jnp.float32)
    for piece in arrived:
        out = out + piece.astype(jnp.float32)
    return out


def on_device(tokens, cotangent, lengths, item_rows, w_in, w_out, table, moment_one, moment_two):
    wide, narrow = lax.axis_size("wide"), lax.axis_size("narrow")
    rows_dev, width = table.shape
    cores, inner, pairs, outer = layout_of(wide, narrow)
    held = local_rows(wide, narrow, rows_dev, tokens, cotangent, lengths, item_rows, w_in, w_out)
    plane = inner * pairs
    stages = (
        ([(c, 0, 0, 0) for c in range(cores)], range(1, cores)),
        ([(0, i, y, 0) for i in range(inner) for y in range(pairs)], [plane - 1, *range(1, plane - 1)]),
        ([(0, 0, 0, z) for z in range(outer)], [1, *range(outer - 1, 1, -1)] if outer > 1 else []),
    )
    for number, (offsets, order) in enumerate(stages):
        if number:
            held = held.astype(jnp.bfloat16).reshape(len(offsets), -1, width)
        held = gather_sum(held, offsets, order, wide, narrow)
    return adam_rows(held, table, moment_one, moment_two)


def solution(mesh):
    return jax.shard_map(
        on_device,
        mesh=mesh,
        in_specs=(
            P(AXES, None, None),
            P(AXES, None, None),
            P(AXES),
            P(AXES, None),
            P(),
            P(),
            P(AXES, None),
            P(AXES, None),
            P(AXES, None),
        ),
        out_specs=(P(AXES, None), P(AXES, None), P(AXES, None)),
        check_vma=False,
    )
```

time: 36.2 us -> 32.6 us (0.901)
  Pallas kernels: 12.5 us -> 9.66 us
  waiting for transfers between devices: 11.8 us -> 10.3 us
  starting transfers between devices: 9.85 us -> 10.6 us
    pallas_call x1, Pallas kernels: 12.5 us -> 9.66 us  [local_rows(): pl.pallas_call(functools.partial(local_kernel, wide, narrow, rows_dev), o...]
    ppermute x7, waiting for transfers between devices: 11.8 us -> 10.3 us  [send(): return lax.ppermute(x, AXES, perm)]
    ppermute x7, starting transfers between devices: 9.85 us -> 10.6 us  [send(): return lax.ppermute(x, AXES, perm)]
where the time goes in v3:
time: 32.6 us; the launch traced here: 32.5 us
  starting transfers between devices  10.6 us (33%)
  waiting for transfers between devices  10.3 us (32%)
  Pallas kernels  9.66 us (30%)
  other arithmetic  1.12 us (3%)
  between operations  0.71 us (2%)
    ppermute x7, starting transfers between devices, send(): return lax.ppermute(x, AXES, perm)  10.6 us
    ppermute x7, waiting for transfers between devices, send(): return lax.ppermute(x, AXES, perm)  10.3 us
    pallas_call x1, Pallas kernels, local_rows(): pl.pallas_call(functools.partial(local_kernel, wide, narrow, rows_dev), o...  9.66 us
    sub x1, other arithmetic, adam_rows(): table - step_size * first_moment / scaled  0.78 us
  transfers between devices with their start and end apart: 7, of which 6 were waited for; matrix products, arithmetic and copies ran while one was open for 0% of the time, Pallas kernels for 0%

profile of v3, /device:TPU:0, one launch (start us, length us, event | category | flops | bytes accessed | tf_op | source)
XLA Modules:
  0.0 32.5 jit_solution(1732834935237574045)
XLA Ops:
  0.6 9.7 %local_rows.1 = (bf16[512,512]{1,0:T(8,128)(2,1)S(1)}, bf16[512,512]{1,0:T(8,128)(2,1)S(1)}) custom-call(s32[2]{0:T(128)} %len_hbm.1, s32[2,256]{1,0:T(2,128)} %rows_hbm.1, bf16[2,256,512]{2,1,0:T(8,128)(2,1)} %tok_hbm.1, bf16[2,256,512]{2,1,0:T(8,128)(2,1)} %cot_hbm.1, bf16[512,2048]{1,0:T(8,128)(2,1)} %win_hbm.1, bf16[512,512]{1,0:T(8,128)(2,1)} %wout_hbm.1), custom_call_target="tpu_custom_call" | custom-call | flops 2952790016 | bytes 4718592 | tf_op jit(solution)/shard_map/local_rows/pallas_call | solution.py:260
  10.3 0.0 copy-start
  10.3 0.0 copy-start.1
  10.3 0.0 copy-start.2
  10.3 0.5 %collective-permute-start = (bf16[512,512]{1,0:T(8,128)(2,1)S(1)}, bf16[512,512]{1,0:T(8,128)(2,1)S(1)}, u32[]{:S(2)}, u32[]{:S(2)}) collective-permute-start(bf16[512,512]{1,0:T(8,128)(2,1)S(1)} %get-tuple-element.6), channel_id=1, source_target_pairs={{0,1},{1,0},{2,3},{3,2},{4,5},{5,4},{6,7},{7,6},{8,9},{9,8},{10,11... | collective-permute-start | bytes 1572872 | tf_op jit(solution)/shard_map/ppermute | solution.py:46
  10.9 1.5 %collective-permute-done = bf16[512,512]{1,0:T(8,128)(2,1)S(1)} collective-permute-done((bf16[512,512]{1,0:T(8,128)(2,1)S(1)}, bf16[512,512]{1,0:T(8,128)(2,1)S(1)}, u32[]{:S(2)}, u32[]{:S(2)}) %collective-permute-start) | collective-permute-done | bytes 524320 | tf_op jit(solution)/shard_map/ppermute | solution.py:46
  12.4 0.1 add_convert_fusion
  12.6 3.9 %collective-permute-start.1 = (bf16[128,512]{1,0:T(8,128)(2,1)S(1)}, bf16[128,512]{1,0:T(8,128)(2,1)S(1)}, u32[]{:S(2)}, u32[]{:S(2)}) collective-permute-start(bf16[128,512]{1,0:T(8,128)(2,1)S(1)} %get-tuple-element.10), channel_id=1, source_target_pairs={{0,6},{1,7},{2,4},{3,5},{4,2},{5,3},{6,0},{7,1},{8,14},{9,15},{10,... | collective-permute-start | bytes 393224 | tf_op jit(solution)/shard_map/ppermute | solution.py:46
  16.5 0.5 %collective-permute-start.3 = (bf16[128,512]{1,0:T(8,128)(2,1)S(1)}, bf16[128,512]{1,0:T(8,128)(2,1)S(1)}, u32[]{:S(2)}, u32[]{:S(2)}) collective-permute-start(bf16[128,512]{1,0:T(8,128)(2,1)S(1)} %get-tuple-element.11), channel_id=1, source_target_pairs={{0,4},{1,5},{2,6},{3,7},{4,0},{5,1},{6,2},{7,3},{8,12},{9,13},{10,... | collective-permute-start | bytes 393224 | tf_op jit(solution)/shard_map/ppermute | solution.py:46
  17.0 0.1 collective-permute-start.2
  17.1 3.7 %collective-permute-done.1 = bf16[128,512]{1,0:T(8,128)(2,1)S(1)} collective-permute-done((bf16[128,512]{1,0:T(8,128)(2,1)S(1)}, bf16[128,512]{1,0:T(8,128)(2,1)S(1)}, u32[]{:S(2)}, u32[]{:S(2)}) %collective-permute-start.1) | collective-permute-done | bytes 131104 | tf_op jit(solution)/shard_map/ppermute | solution.py:46
  20.8 2.5 %collective-permute-done.3 = bf16[128,512]{1,0:T(8,128)(2,1)S(1)} collective-permute-done((bf16[128,512]{1,0:T(8,128)(2,1)S(1)}, bf16[128,512]{1,0:T(8,128)(2,1)S(1)}, u32[]{:S(2)}, u32[]{:S(2)}) %collective-permute-start.3) | collective-permute-done | bytes 131104 | tf_op jit(solution)/shard_map/ppermute | solution.py:46
  23.3 0.0 collective-permute-done.2
  23.3 0.1 add_convert_fusion.1
  23.4 1.6 %collective-permute-start.4 = (bf16[32,512]{1,0:T(8,128)(2,1)S(1)}, bf16[32,512]{1,0:T(8,128)(2,1)S(1)}, u32[]{:S(2)}, u32[]{:S(2)}) collective-permute-start(bf16[32,512]{1,0:T(8,128)(2,1)S(1)} %get-tuple-element.13), channel_id=1, source_target_pairs={{0,8},{1,9},{2,10},{3,11},{4,12},{5,13},{6,14},{7,15},{8,16},{9,17... | collective-permute-start | bytes 98312 | tf_op jit(solution)/shard_map/ppermute | solution.py:46
  25.0 2.6 %collective-permute-start.6 = (bf16[32,512]{1,0:T(8,128)(2,1)S(1)}, bf16[32,512]{1,0:T(8,128)(2,1)S(1)}, u32[]{:S(2)}, u32[]{:S(2)}) collective-permute-start(bf16[32,512]{1,0:T(8,128)(2,1)S(1)} %get-tuple-element.14), channel_id=1, source_target_pairs={{0,16},{1,17},{2,18},{3,19},{4,20},{5,21},{6,22},{7,23},{8,24},{9,... | collective-permute-start | bytes 98312 | tf_op jit(solution)/shard_map/ppermute | solution.py:46
  27.6 1.3 %collective-permute-start.5 = (bf16[32,512]{1,0:T(8,128)(2,1)S(1)}, bf16[32,512]{1,0:T(8,128)(2,1)S(1)}, u32[]{:S(2)}, u32[]{:S(2)}) collective-permute-start(bf16[32,512]{1,0:T(8,128)(2,1)S(1)} %get-tuple-element.15), channel_id=1, source_target_pairs={{0,24},{1,25},{2,26},{3,27},{4,28},{5,29},{6,30},{7,31},{8,0},{9,1... | collective-permute-start | bytes 98312 | tf_op jit(solution)/shard_map/ppermute | solution.py:46
  29.0 0.7 %collective-permute-done.4 = bf16[32,512]{1,0:T(8,128)(2,1)S(1)} collective-permute-done((bf16[32,512]{1,0:T(8,128)(2,1)S(1)}, bf16[32,512]{1,0:T(8,128)(2,1)S(1)}, u32[]{:S(2)}, u32[]{:S(2)}) %collective-permute-start.4) | collective-permute-done | bytes 32800 | tf_op jit(solution)/shard_map/ppermute | solution.py:46
  29.6 0.6 %collective-permute-done.6 = bf16[32,512]{1,0:T(8,128)(2,1)S(1)} collective-permute-done((bf16[32,512]{1,0:T(8,128)(2,1)S(1)}, bf16[32,512]{1,0:T(8,128)(2,1)S(1)}, u32[]{:S(2)}, u32[]{:S(2)}) %collective-permute-start.6) | collective-permute-done | bytes 32800 | tf_op jit(solution)/shard_map/ppermute | solution.py:46
  30.2 1.3 %collective-permute-done.5 = bf16[32,512]{1,0:T(8,128)(2,1)S(1)} collective-permute-done((bf16[32,512]{1,0:T(8,128)(2,1)S(1)}, bf16[32,512]{1,0:T(8,128)(2,1)S(1)}, u32[]{:S(2)}, u32[]{:S(2)}) %collective-permute-start.5) | collective-permute-done | bytes 32800 | tf_op jit(solution)/shard_map/ppermute | solution.py:46
  31.6 0.1 multiply_reduce_fusion
  31.7 0.0 copy-done
  31.7 0.0 copy-done.1
  31.7 0.0 copy-done.2
  31.7 0.8 %divide_subtract_fusion = (f32[32,512]{1,0:T(8,128)}, f32[32,512]{1,0:T(8,128)}, f32[32,512]{1,0:T(8,128)}) fusion(f32[32,512]{1,0:T(8,128)S(1)} %copy-done, f32[32]{0:T(128)S(1)} %maximum_divide_fusion, bf16[32,512]{1,0:T(8,128)(2,1)S(1)} %collective-permute-done.6, bf16[32,512]{1,0:T(8,128)(2,1)S(1)} %collective-permute-done.5, ...), kind=kLoop, calls=%fused_computation.4 | loop fusion | flops 327680 | bytes 524416 | tf_op jit(solution)/shard_map/sub | solution.py:299
  (3 shorter events, 0.0 us)
Async XLA Ops:
  10.3 21.4 %copy-start = (f32[32,512]{1,0:T(8,128)S(1)}, f32[32,512]{1,0:T(8,128)}, u32[]{:S(2)}) copy-start(f32[32,512]{1,0:T(8,128)} %param.15) | copy-start | bytes 196612
  10.3 21.4 %copy-start.1 = (f32[32,512]{1,0:T(8,128)S(1)}, f32[32,512]{1,0:T(8,128)}, u32[]{:S(2)}) copy-start(f32[32,512]{1,0:T(8,128)} %param.16) | copy-start | bytes 196612
  10.3 21.4 %copy-start.2 = (f32[32,512]{1,0:T(8,128)S(1)}, f32[32,512]{1,0:T(8,128)}, u32[]{:S(2)}) copy-start(f32[32,512]{1,0:T(8,128)} %param.17) | copy-start | bytes 196612
  10.3 2.1 %collective-permute-start = (bf16[512,512]{1,0:T(8,128)(2,1)S(1)}, bf16[512,512]{1,0:T(8,128)(2,1)S(1)}, u32[]{:S(2)}, u32[]{:S(2)}) collective-permute-start(bf16[512,512]{1,0:T(8,128)(2,1)S(1)} %get-tuple-element.6), channel_id=1, source_target_pairs={{0,1},{1,0},{2,3},{3,2},{4,5},{5,4},{6,7},{7,6},{8,9},{9,8},{10,11... | collective-permute-start | bytes 1572872 | tf_op jit(solution)/shard_map/ppermute | solution.py:46
  12.6 8.2 %collective-permute-start.1 = (bf16[128,512]{1,0:T(8,128)(2,1)S(1)}, bf16[128,512]{1,0:T(8,128)(2,1)S(1)}, u32[]{:S(2)}, u32[]{:S(2)}) collective-permute-start(bf16[128,512]{1,0:T(8,128)(2,1)S(1)} %get-tuple-element.10), channel_id=1, source_target_pairs={{0,6},{1,7},{2,4},{3,5},{4,2},{5,3},{6,0},{7,1},{8,14},{9,15},{10,... | collective-permute-start | bytes 393224 | tf_op jit(solution)/shard_map/ppermute | solution.py:46
  16.5 6.9 %collective-permute-start.3 = (bf16[128,512]{1,0:T(8,128)(2,1)S(1)}, bf16[128,512]{1,0:T(8,128)(2,1)S(1)}, u32[]{:S(2)}, u32[]{:S(2)}) collective-permute-start(bf16[128,512]{1,0:T(8,128)(2,1)S(1)} %get-tuple-element.11), channel_id=1, source_target_pairs={{0,4},{1,5},{2,6},{3,7},{4,0},{5,1},{6,2},{7,3},{8,12},{9,13},{10,... | collective-permute-start | bytes 393224 | tf_op jit(solution)/shard_map/ppermute | solution.py:46
  17.0 6.3 %collective-permute-start.2 = (bf16[128,512]{1,0:T(8,128)(2,1)S(1)}, bf16[128,512]{1,0:T(8,128)(2,1)S(1)}, u32[]{:S(2)}, u32[]{:S(2)}) collective-permute-start(bf16[128,512]{1,0:T(8,128)(2,1)S(1)} %get-tuple-element.12), channel_id=1, source_target_pairs={{0,2},{1,3},{2,0},{3,1},{4,6},{5,7},{6,4},{7,5},{8,10},{9,11},{10,... | collective-permute-start | bytes 393224 | tf_op jit(solution)/shard_map/ppermute | solution.py:46
  23.4 6.2 %collective-permute-start.4 = (bf16[32,512]{1,0:T(8,128)(2,1)S(1)}, bf16[32,512]{1,0:T(8,128)(2,1)S(1)}, u32[]{:S(2)}, u32[]{:S(2)}) collective-permute-start(bf16[32,512]{1,0:T(8,128)(2,1)S(1)} %get-tuple-element.13), channel_id=1, source_target_pairs={{0,8},{1,9},{2,10},{3,11},{4,12},{5,13},{6,14},{7,15},{8,16},{9,17... | collective-permute-start | bytes 98312 | tf_op jit(solution)/shard_map/ppermute | solution.py:46
  25.0 5.2 %collective-permute-start.6 = (bf16[32,512]{1,0:T(8,128)(2,1)S(1)}, bf16[32,512]{1,0:T(8,128)(2,1)S(1)}, u32[]{:S(2)}, u32[]{:S(2)}) collective-permute-start(bf16[32,512]{1,0:T(8,128)(2,1)S(1)} %get-tuple-element.14), channel_id=1, source_target_pairs={{0,16},{1,17},{2,18},{3,19},{4,20},{5,21},{6,22},{7,23},{8,24},{9,... | collective-permute-start | bytes 98312 | tf_op jit(solution)/shard_map/ppermute | solution.py:46
  27.6 3.9 %collective-permute-start.5 = (bf16[32,512]{1,0:T(8,128)(2,1)S(1)}, bf16[32,512]{1,0:T(8,128)(2,1)S(1)}, u32[]{:S(2)}, u32[]{:S(2)}) collective-permute-start(bf16[32,512]{1,0:T(8,128)(2,1)S(1)} %get-tuple-element.15), channel_id=1, source_target_pairs={{0,24},{1,25},{2,26},{3,27},{4,28},{5,29},{6,30},{7,31},{8,0},{9,1... | collective-permute-start | bytes 98312 | tf_op jit(solution)/shard_map/ppermute | solution.py:46

commit v4 on v3

--- a/solution.py
+++ b/solution.py
@@ -28,12 +28,16 @@
     return cores, inner, narrow // cores, wide // inner
 
 
+def shifted(at, by, size):
+    return at ^ by if size & (size - 1) == 0 else (at + by) % size
+
+
 def destination(wide, narrow, w, n, cr, ir, yr, zr):
     cores, inner, pairs, outer = layout_of(wide, narrow)
     z, i = w // inner, w % inner
     y, c = n // cores, n % cores
-    w_to = ((z + zr) % outer) * inner + (i + ir) % inner
-    n_to = ((y + yr) % pairs) * cores + (c + cr) % cores
+    w_to = shifted(z, zr, outer) * inner + shifted(i, ir, inner)
+    n_to = shifted(y, yr, pairs) * cores + shifted(c, cr, cores)
     return w_to, n_to
 
 
@@ -58,7 +62,7 @@
     wide, narrow, rows_dev,
     len_hbm, rows_hbm, tok_hbm, cot_hbm, win_hbm, wout_hbm,
     keep_ref, send_ref,
-    len_ref, rows_ref, tok, cot, win, wout, hid, slope, att, fac, mixed, inner_grad, dgated, dm_s, sems,
+    len_ref, rows_ref, tok, cot, win, wout, hid, slope, att, fac, mixed, inner_grad, dgated, grads, dm_s, sems,
 ):
     micro, lmax, width = tok_hbm.shape
     half = lmax // 2
@@ -77,6 +81,15 @@
     row = lax.broadcasted_iota(jnp.int32, (lmax, 1), 0)
     copies[0].wait()
     source = tok[...].reshape(total, width) * jnp.asarray(0.5, bf16)
+
+    def activate(u, cols):
+        th = jnp.tanh(u)
+        up = 1.0 + th
+        act = u * up
+        hid[:, cols] = act.astype(bf16)
+        slope[:, cols] = up + act * (1.0 - th)
+
+    waiting = ()
     for part, (lo, hi) in enumerate(zip(bounds, bounds[1:])):
         copies[1 + part].wait()
         if hi == 4 * width:
@@ -88,12 +101,11 @@
         for first in range(lo, hi, tile):
             cols = pl.ds(first, tile)
             u = dot(source, win[:, cols])
-            th = jnp.tanh(u)
-            up = 1.0 + th
-            act = u * up
-            hid[:, cols] = act.astype(bf16)
-            slope[:, cols] = up + act * (1.0 - th)
-    dgated[...] = dot_nt(cot[...].reshape(total, width), wout[...]).astype(bf16)
+            if waiting:
+                activate(*waiting)
+            waiting = (u, cols)
+    dgated[...] = dot_nt(cot[...].reshape(total, width), wout[...])
+    activate(*waiting)
 
     lane = lax.broadcasted_iota(jnp.int32, (1, LANES), 1)
     heads_here = LANES // per_head
@@ -101,6 +113,7 @@
     scale = per_head ** (-0.5)
     causal = lax.broadcasted_iota(jnp.int32, (half, half), 1) <= lax.broadcasted_iota(jnp.int32, (half, half), 0)
     none = jnp.zeros((half, half), bf16)
+    far = -1e4
     lane_pairs = width // LANES
     group = 32
     groups = lmax // group
@@ -113,9 +126,6 @@
 
     def forward_pair(s, p):
         here = pl.ds(s * lmax, lmax)
-        length = len_ref[s]
-        share = jnp.where(row < length, 1.0 / jnp.full((lmax, 1), length, jnp.int32).astype(f32), 0.0)
-        share_half = share * (0.5 * scale)
         q = hid[here, pl.ds(2 * width + p * LANES, LANES)]
         k = hid[here, pl.ds(3 * width + p * LANES, LANES)]
         v = hid[here, pl.ds(width + p * LANES, LANES)]
@@ -127,19 +137,21 @@
             parts = []
             for b in range(2):
                 rows = slice(b * half, (b + 1) * half)
-                u = scores[h * lmax + b * half : h * lmax + (b + 1) * half, : (b + 1) * half]
-                th = jnp.tanh(u)
-                up = 1.0 + th
-                act = u * up
-                w_b = act * share[rows]
-                f_b = (up + act * (1.0 - th)) * share_half[rows]
-                diag = jnp.where(causal, w_b[:, rows], 0.0).astype(bf16)
-                fac[s, head, rows, rows] = jnp.where(causal, f_b[:, rows], 0.0)
+                first = h * lmax + b * half
+                pieces = []
+                for c in range(b + 1):
+                    cols = slice(c * half, (c + 1) * half)
+                    u = scores[first : first + half, cols]
+                    if c == b:
+                        u = jnp.where(causal, u, far)
+                    th = jnp.tanh(u)
+                    up = 1.0 + th
+                    act = u * up
+                    fac[s, head, rows, cols] = up + act * (1.0 - th)
+                    pieces.append(act.astype(bf16))
                 if b == 0:
-                    parts.append(jnp.concatenate([diag, none], axis=1))
-                else:
-                    fac[s, head, rows, :half] = f_b[:, :half]
-                    parts.append(jnp.concatenate([w_b[:, :half].astype(bf16), diag], axis=1))
+                    pieces.append(none)
+                parts.append(jnp.concatenate(pieces, axis=1))
             weight = jnp.concatenate(parts, axis=0)
             att[s, head] = weight
             weights.append(weight)
@@ -148,17 +160,20 @@
     def norm_group(s, r):
         rows = pl.ds(r * group, group)
         those = pl.ds(s * lmax + r * group, group)
-        mix = mixed[s, rows, :]
+        length = len_ref[s]
+        place = lax.broadcasted_iota(jnp.int32, (group, 1), 0) + r * group
+        share = jnp.where(place < length, 1.0 / jnp.full((group, 1), length, jnp.int32).astype(f32), 0.0)
+        mix = mixed[s, rows, :] * share
         centered = mix - jnp.mean(mix, axis=1, keepdims=True)
         inv = lax.rsqrt(jnp.mean(centered * centered, axis=1, keepdims=True) + norm_eps)
         normed = centered * inv
-        dg = dgated[those, :].astype(f32)
+        dg = dgated[those, :]
         gate = hid[those, pl.ds(0, width)].astype(f32)
-        dgate = (dg * normed).astype(bf16).astype(f32)
-        inner_grad[those, pl.ds(0, width)] = (dgate * slope[those, pl.ds(0, width)]).astype(bf16)
+        dgn = dg * normed
+        inner_grad[those, pl.ds(0, width)] = (dgn * slope[those, pl.ds(0, width)]).astype(bf16)
         dn = dg * gate
-        dmix = inv * (
-            dn - jnp.mean(dn, axis=1, keepdims=True) - normed * jnp.mean(dn * normed, axis=1, keepdims=True)
+        dmix = (inv * share) * (
+            dn - jnp.mean(dn, axis=1, keepdims=True) - normed * jnp.mean(dgn * gate, axis=1, keepdims=True)
         )
         dm_s[s, rows, :] = dmix.astype(bf16)
 
@@ -170,22 +185,21 @@
         v = hid[here, pl.ds(width + p * LANES, LANES)]
         dmp = dm_s[s, :, lanes]
         dm_t = dmp.T
-        d_att = dot_nt(jnp.concatenate([dmp * m for m in masks], axis=0), v)
+        small = jnp.asarray(0.5 * scale, bf16)
+        d_att = dot_nt(jnp.concatenate([dmp * (m * small) for m in masks], axis=0), v)
         stacked, dks, dvs = [], [], []
         for h in range(heads_here):
             head = p * heads_here + h
             feat = slice(h * per_head, (h + 1) * per_head)
             dvs.append(dot(dm_t[feat], att[s, head]).astype(bf16))
-            d_top = d_att[h * lmax : h * lmax + half, :half].astype(bf16).astype(f32)
-            d_low = d_att[h * lmax + half : (h + 1) * lmax].astype(bf16).astype(f32)
-            ds_top = (d_top * fac[s, head, :half, :half]).astype(bf16)
-            ds_low = (d_low * fac[s, head, half:, :]).astype(bf16)
+            ds_top = (d_att[h * lmax : h * lmax + half, :half] * fac[s, head, :half, :half]).astype(bf16)
+            ds_low = (d_att[h * lmax + half : (h + 1) * lmax] * fac[s, head, half:, :]).astype(bf16)
             ds = jnp.concatenate([jnp.concatenate([ds_top, none], axis=1), ds_low], axis=0)
             stacked.append(ds)
             dks.append(dot(q_t[feat], ds).astype(bf16))
         dv = jnp.concatenate(dvs, axis=0).T.astype(f32)
         dk = jnp.concatenate(dks, axis=0).T.astype(f32)
-        dq = pick_lanes(dot(jnp.concatenate(stacked, axis=0), k)).astype(bf16).astype(f32)
+        dq = pick_lanes(dot(jnp.concatenate(stacked, axis=0), k))
         for part, piece in ((1, dv), (2, dq), (3, dk)):
             cols = pl.ds(part * width + p * LANES, LANES)
             inner_grad[here, cols] = (piece * slope[here, cols]).astype(bf16)
@@ -210,14 +224,11 @@
     for p in range(lane_pairs):
         backward_pair(micro - 1, p)
 
-    back = (0.5 * dot_nt(inner_grad[...], win[...])).astype(bf16).astype(f32)
-    grads = (back + cot[...].reshape(total, width).astype(f32)).astype(bf16)
-    dgated[...] = grads
+    back = 0.5 * dot_nt(inner_grad[...], win[...])
+    grads[...] = (back + cot[...].reshape(total, width).astype(f32)).astype(bf16)
 
     cores, inner_w, pairs, outer = layout_of(wide, narrow)
     w_me, n_me = lax.axis_index("wide"), lax.axis_index("narrow")
-    z_me, i_me = w_me // inner_w, w_me % inner_w
-    y_me, c_me = n_me // cores, n_me % cores
     blocks = wide * narrow // cores
     per_chunk = min(8, blocks)
     size = per_chunk * rows_dev
@@ -231,16 +242,15 @@
                 zr = block % outer
                 yr = (block // outer) % pairs
                 ir = block // (outer * pairs)
-                w_to = ((z_me + zr) % outer) * inner_w + (i_me + ir) % inner_w
-                n_to = ((y_me + yr) % pairs) * cores + (c_me + core_offset) % cores
-                want = slot + (w_to * narrow + n_to) * rows_dev
+                w_to, n_to = destination(wide, narrow, w_me, n_me, core_offset, ir, yr, zr)
+                first = (w_to * narrow + n_to) * rows_dev
                 pieces.append(
                     jnp.concatenate(
-                        [(want == rows_ref[s : s + 1, :]).astype(f32).astype(bf16) for s in range(micro)], axis=1
+                        [(slot == rows_ref[s : s + 1, :] - first).astype(f32).astype(bf16) for s in range(micro)], axis=1
                     )
                 )
             chosen = jnp.concatenate(pieces, axis=0)
-            out_ref[pl.ds(pl.multiple_of(j * size, size), size), :] = dot(chosen, dgated[...]).astype(bf16)
+            out_ref[pl.ds(pl.multiple_of(j * size, size), size), :] = dot(chosen, grads[...]).astype(bf16)
             return carry
 
         lax.fori_loop(0, blocks // per_chunk, one_chunk, 0, unroll=blocks // per_chunk <= 4)
@@ -275,6 +285,7 @@
             pltpu.VMEM((micro, HEADS, lmax, lmax), f32),
             pltpu.VMEM((micro, lmax, width), f32),
             pltpu.VMEM((total, 4 * width), bf16),
+            pltpu.VMEM((total, width), f32),
             pltpu.VMEM((total, width), bf16),
             pltpu.VMEM((micro, lmax, width), bf16),
             pltpu.SemaphoreType.DMA((8,)),
@@ -311,17 +322,19 @@
     wide, narrow = lax.axis_size("wide"), lax.axis_size("narrow")
     rows_dev, width = table.shape
     cores, inner, pairs, outer = layout_of(wide, narrow)
-    held = local_rows(wide, narrow, rows_dev, tokens, cotangent, lengths, item_rows, w_in, w_out)
-    plane = inner * pairs
-    stages = (
-        ([(c, 0, 0, 0) for c in range(cores)], range(1, cores)),
-        ([(0, i, y, 0) for i in range(inner) for y in range(pairs)], [plane - 1, *range(1, plane - 1)]),
-        ([(0, 0, 0, z) for z in range(outer)], [1, *range(outer - 1, 1, -1)] if outer > 1 else []),
-    )
-    for number, (offsets, order) in enumerate(stages):
-        if number:
-            held = held.astype(jnp.bfloat16).reshape(len(offsets), -1, width)
-        held = gather_sum(held, offsets, order, wide, narrow)
+    blocks = local_rows(wide, narrow, rows_dev, tokens, cotangent, lengths, item_rows, w_in, w_out)
+    held = gather_sum(blocks, [(c, 0, 0, 0) for c in range(cores)], range(1, cores), wide, narrow)
+    held = held.astype(jnp.bfloat16).reshape(inner * pairs, outer, rows_dev, width)
+    plane = [(0, i, y, 0) for i in range(inner) for y in range(pairs)]
+    cut = outer // 2
+    summed = {}
+    for lo, hi in ((cut, outer), (0, cut)):
+        pieces = [held[k, lo:hi].reshape(-1, width) for k in range(len(plane))]
+        part = gather_sum(pieces, plane, range(1, len(plane)), wide, narrow).reshape(hi - lo, rows_dev, width)
+        summed.update({z: part[z - lo] for z in range(lo, hi)})
+    order = [*range(cut, outer), *range(cut - 1, 0, -1)]
+    pieces = [summed[z].astype(jnp.bfloat16) if z else summed[z] for z in range(outer)]
+    held = gather_sum(pieces, [(0, 0, 0, z) for z in range(outer)], order, wide, narrow)
     return adam_rows(held, table, moment_one, moment_two)
 
 

time: 32.6 us -> 31.3 us (0.960)
  waiting for transfers between devices: 10.3 us -> 6.51 us
  starting transfers between devices: 10.6 us -> 13.2 us
    ppermute x7 -> x10, waiting for transfers between devices: 10.3 us -> 6.51 us  [send(): return lax.ppermute(x, AXES, perm)]
    ppermute x7 -> x10, starting transfers between devices: 10.6 us -> 13.2 us  [send(): return lax.ppermute(x, AXES, perm)]
  transfers between devices with their start and end apart: 7 -> 10, of which waited for: 6 -> 5; matrix products, arithmetic and copies ran while one was open for 0% -> 0% of each run, Pallas kernels for 0% -> 0%
where the time goes in v4:
time: 31.3 us; the launch traced here: 31.1 us
  starting transfers between devices  13.2 us (42%)
  Pallas kernels  9.51 us (30%)
  waiting for transfers between devices  6.51 us (21%)
  other arithmetic  1.13 us (4%)
  between operations  0.73 us (2%)
    ppermute x10, starting transfers between devices, send(): return lax.ppermute(x, AXES, perm)  13.2 us
    pallas_call x1, Pallas kernels, local_rows(): pl.pallas_call(functools.partial(local_kernel, wide, narrow, rows_dev), o...  9.51 us
    ppermute x10, waiting for transfers between devices, send(): return lax.ppermute(x, AXES, perm)  6.51 us
    sub x1, other arithmetic, adam_rows(): table - step_size * first_moment / scaled  0.77 us
  transfers between devices with their start and end apart: 10, of which 5 were waited for; matrix products, arithmetic and copies ran while one was open for 0% of the time, Pallas kernels for 0%

profile of v4, /device:TPU:0, one launch (start us, length us, event | category | flops | bytes accessed | tf_op | source)
XLA Modules:
  0.0 31.1 jit_solution(16334630364216272170)
XLA Ops:
  0.6 9.5 %local_rows.1 = (bf16[512,512]{1,0:T(8,128)(2,1)S(1)}, bf16[512,512]{1,0:T(8,128)(2,1)S(1)}) custom-call(s32[2]{0:T(128)} %len_hbm.1, s32[2,256]{1,0:T(2,128)} %rows_hbm.1, bf16[2,256,512]{2,1,0:T(8,128)(2,1)} %tok_hbm.1, bf16[2,256,512]{2,1,0:T(8,128)(2,1)} %cot_hbm.1, bf16[512,2048]{1,0:T(8,128)(2,1)} %win_hbm.1, bf16[512,512]{1,0:T(8,128)(2,1)} %wout_hbm.1), custom_call_target="tpu_custom_call" | custom-call | flops 2952790016 | bytes 4718592 | tf_op jit(solution)/shard_map/local_rows/pallas_call | solution.py:270
  10.1 0.0 copy-start
  10.2 0.0 copy-start.1
  10.2 0.0 copy-start.2
  10.2 0.6 %collective-permute-start = (bf16[512,512]{1,0:T(8,128)(2,1)S(1)}, bf16[512,512]{1,0:T(8,128)(2,1)S(1)}, u32[]{:S(2)}, u32[]{:S(2)}) collective-permute-start(bf16[512,512]{1,0:T(8,128)(2,1)S(1)} %get-tuple-element.6), channel_id=1, source_target_pairs={{0,1},{1,0},{2,3},{3,2},{4,5},{5,4},{6,7},{7,6},{8,9},{9,8},{10,11... | collective-permute-start | bytes 1572872 | tf_op jit(solution)/shard_map/ppermute | solution.py:50
  10.7 1.5 %collective-permute-done = bf16[512,512]{1,0:T(8,128)(2,1)S(1)} collective-permute-done((bf16[512,512]{1,0:T(8,128)(2,1)S(1)}, bf16[512,512]{1,0:T(8,128)(2,1)S(1)}, u32[]{:S(2)}, u32[]{:S(2)}) %collective-permute-start) | collective-permute-done | bytes 524320 | tf_op jit(solution)/shard_map/ppermute | solution.py:50
  12.3 0.1 add_convert_fusion
  12.5 3.9 %collective-permute-start.6 = (bf16[64,512]{1,0:T(8,128)(2,1)S(1)}, bf16[64,512]{1,0:T(8,128)(2,1)S(1)}, u32[]{:S(2)}, u32[]{:S(2)}) collective-permute-start(bf16[64,512]{1,0:T(8,128)(2,1)S(1)} %bitcast.19), channel_id=1, source_target_pairs={{0,6},{1,7},{2,4},{3,5},{4,2},{5,3},{6,0},{7,1},{8,14},{9,15},{10,... | collective-permute-start | bytes 196616 | tf_op jit(solution)/shard_map/ppermute | solution.py:50
  16.3 0.5 %collective-permute-start.5 = (bf16[64,512]{1,0:T(8,128)(2,1)S(1)}, bf16[64,512]{1,0:T(8,128)(2,1)S(1)}, u32[]{:S(2)}, u32[]{:S(2)}) collective-permute-start(bf16[64,512]{1,0:T(8,128)(2,1)S(1)} %bitcast.18), channel_id=1, source_target_pairs={{0,4},{1,5},{2,6},{3,7},{4,0},{5,1},{6,2},{7,3},{8,12},{9,13},{10,... | collective-permute-start | bytes 196616 | tf_op jit(solution)/shard_map/ppermute | solution.py:50
  16.9 0.1 collective-permute-start.4
  17.0 2.8 %collective-permute-start.3 = (bf16[64,512]{1,0:T(8,128)(2,1)S(1)}, bf16[64,512]{1,0:T(8,128)(2,1)S(1)}, u32[]{:S(2)}, u32[]{:S(2)}) collective-permute-start(bf16[64,512]{1,0:T(8,128)(2,1)S(1)} %bitcast.16), channel_id=1, source_target_pairs={{0,6},{1,7},{2,4},{3,5},{4,2},{5,3},{6,0},{7,1},{8,14},{9,15},{10,... | collective-permute-start | bytes 196616 | tf_op jit(solution)/shard_map/ppermute | solution.py:50
  19.8 0.5 %collective-permute-start.2 = (bf16[64,512]{1,0:T(8,128)(2,1)S(1)}, bf16[64,512]{1,0:T(8,128)(2,1)S(1)}, u32[]{:S(2)}, u32[]{:S(2)}) collective-permute-start(bf16[64,512]{1,0:T(8,128)(2,1)S(1)} %bitcast.15), channel_id=1, source_target_pairs={{0,4},{1,5},{2,6},{3,7},{4,0},{5,1},{6,2},{7,3},{8,12},{9,13},{10,... | collective-permute-start | bytes 196616 | tf_op jit(solution)/shard_map/ppermute | solution.py:50
  20.4 0.0 collective-permute-done.6
  20.4 0.5 %collective-permute-start.1 = (bf16[64,512]{1,0:T(8,128)(2,1)S(1)}, bf16[64,512]{1,0:T(8,128)(2,1)S(1)}, u32[]{:S(2)}, u32[]{:S(2)}) collective-permute-start(bf16[64,512]{1,0:T(8,128)(2,1)S(1)} %bitcast.14), channel_id=1, source_target_pairs={{0,2},{1,3},{2,0},{3,1},{4,6},{5,7},{6,4},{7,5},{8,10},{9,11},{10,... | collective-permute-start | bytes 196616 | tf_op jit(solution)/shard_map/ppermute | solution.py:50
  20.9 0.1 collective-permute-done.5
  21.0 1.0 %collective-permute-done.4 = bf16[64,512]{1,0:T(8,128)(2,1)S(1)} collective-permute-done((bf16[64,512]{1,0:T(8,128)(2,1)S(1)}, bf16[64,512]{1,0:T(8,128)(2,1)S(1)}, u32[]{:S(2)}, u32[]{:S(2)}) %collective-permute-start.4) | collective-permute-done | bytes 65568 | tf_op jit(solution)/shard_map/ppermute | solution.py:50
  22.1 2.3 %collective-permute-start.7 = (bf16[32,512]{1,0:T(8,128)(2,1)S(1)}, bf16[32,512]{1,0:T(8,128)(2,1)S(1)}, u32[]{:S(2)}, u32[]{:S(2)}) collective-permute-start(bf16[32,512]{1,0:T(8,128)(2,1)S(1)} %get-tuple-element.20), channel_id=1, source_target_pairs={{0,16},{1,17},{2,18},{3,19},{4,20},{5,21},{6,22},{7,23},{8,24},{9,... | collective-permute-start | bytes 98312 | tf_op jit(solution)/shard_map/ppermute | solution.py:50
  24.4 1.4 %collective-permute-start.8 = (bf16[32,512]{1,0:T(8,128)(2,1)S(1)}, bf16[32,512]{1,0:T(8,128)(2,1)S(1)}, u32[]{:S(2)}, u32[]{:S(2)}) collective-permute-start(bf16[32,512]{1,0:T(8,128)(2,1)S(1)} %get-tuple-element.21), channel_id=1, source_target_pairs={{0,24},{1,25},{2,26},{3,27},{4,28},{5,29},{6,30},{7,31},{8,16},{9,... | collective-permute-start | bytes 98312 | tf_op jit(solution)/shard_map/ppermute | solution.py:50
  25.8 0.0 collective-permute-done.3
  25.8 0.0 collective-permute-done.2
  25.8 0.0 collective-permute-done.1
  25.9 0.5 %collective-permute-start.9 = (bf16[32,512]{1,0:T(8,128)(2,1)S(1)}, bf16[32,512]{1,0:T(8,128)(2,1)S(1)}, u32[]{:S(2)}, u32[]{:S(2)}) collective-permute-start(bf16[32,512]{1,0:T(8,128)(2,1)S(1)} %slice.73), channel_id=1, source_target_pairs={{0,8},{1,9},{2,10},{3,11},{4,12},{5,13},{6,14},{7,15},{8,0},{9,1},... | collective-permute-start | bytes 98312 | tf_op jit(solution)/shard_map/ppermute | solution.py:50
  26.3 1.0 %collective-permute-done.7 = bf16[32,512]{1,0:T(8,128)(2,1)S(1)} collective-permute-done((bf16[32,512]{1,0:T(8,128)(2,1)S(1)}, bf16[32,512]{1,0:T(8,128)(2,1)S(1)}, u32[]{:S(2)}, u32[]{:S(2)}) %collective-permute-start.7) | collective-permute-done | bytes 32800 | tf_op jit(solution)/shard_map/ppermute | solution.py:50
  27.3 2.9 %collective-permute-done.8 = bf16[32,512]{1,0:T(8,128)(2,1)S(1)} collective-permute-done((bf16[32,512]{1,0:T(8,128)(2,1)S(1)}, bf16[32,512]{1,0:T(8,128)(2,1)S(1)}, u32[]{:S(2)}, u32[]{:S(2)}) %collective-permute-start.8) | collective-permute-done | bytes 32800 | tf_op jit(solution)/shard_map/ppermute | solution.py:50
  30.2 0.0 collective-permute-done.9
  30.2 0.1 multiply_reduce_fusion
  30.3 0.0 copy-done
  30.3 0.0 copy-done.1
  30.4 0.0 copy-done.2
  30.4 0.8 %divide_subtract_fusion = (f32[32,512]{1,0:T(8,128)}, f32[32,512]{1,0:T(8,128)}, f32[32,512]{1,0:T(8,128)}) fusion(f32[32,512]{1,0:T(8,128)S(1)} %copy-done, f32[32,512]{1,0:T(8,128)S(1)} %get-tuple-element.11, f32[32]{0:T(128)S(1)} %maximum_divide_fusion, f32[32,512]{1,0:T(8,128)S(1)} %copy-done.1, f32[32,512]{1,0:T(8,128)S(1)} %copy-done.2), kind=kLoop, calls=%fused_computation.14 | loop fusion | flops 212992 | bytes 458880 | tf_op jit(solution)/shard_map/sub | solution.py:310
  (6 shorter events, 0.1 us)
Async XLA Ops:
  10.1 20.2 %copy-start = (f32[32,512]{1,0:T(8,128)S(1)}, f32[32,512]{1,0:T(8,128)}, u32[]{:S(2)}) copy-start(f32[32,512]{1,0:T(8,128)} %param.15) | copy-start | bytes 196612
  10.2 20.2 %copy-start.1 = (f32[32,512]{1,0:T(8,128)S(1)}, f32[32,512]{1,0:T(8,128)}, u32[]{:S(2)}) copy-start(f32[32,512]{1,0:T(8,128)} %param.16) | copy-start | bytes 196612
  10.2 20.2 %copy-start.2 = (f32[32,512]{1,0:T(8,128)S(1)}, f32[32,512]{1,0:T(8,128)}, u32[]{:S(2)}) copy-start(f32[32,512]{1,0:T(8,128)} %param.17) | copy-start | bytes 196612
  10.2 2.1 %collective-permute-start = (bf16[512,512]{1,0:T(8,128)(2,1)S(1)}, bf16[512,512]{1,0:T(8,128)(2,1)S(1)}, u32[]{:S(2)}, u32[]{:S(2)}) collective-permute-start(bf16[512,512]{1,0:T(8,128)(2,1)S(1)} %get-tuple-element.6), channel_id=1, source_target_pairs={{0,1},{1,0},{2,3},{3,2},{4,5},{5,4},{6,7},{7,6},{8,9},{9,8},{10,11... | collective-permute-start | bytes 1572872 | tf_op jit(solution)/shard_map/ppermute | solution.py:50
  12.5 7.9 %collective-permute-start.6 = (bf16[64,512]{1,0:T(8,128)(2,1)S(1)}, bf16[64,512]{1,0:T(8,128)(2,1)S(1)}, u32[]{:S(2)}, u32[]{:S(2)}) collective-permute-start(bf16[64,512]{1,0:T(8,128)(2,1)S(1)} %bitcast.19), channel_id=1, source_target_pairs={{0,6},{1,7},{2,4},{3,5},{4,2},{5,3},{6,0},{7,1},{8,14},{9,15},{10,... | collective-permute-start | bytes 196616 | tf_op jit(solution)/shard_map/ppermute | solution.py:50
  16.3 4.6 %collective-permute-start.5 = (bf16[64,512]{1,0:T(8,128)(2,1)S(1)}, bf16[64,512]{1,0:T(8,128)(2,1)S(1)}, u32[]{:S(2)}, u32[]{:S(2)}) collective-permute-start(bf16[64,512]{1,0:T(8,128)(2,1)S(1)} %bitcast.18), channel_id=1, source_target_pairs={{0,4},{1,5},{2,6},{3,7},{4,0},{5,1},{6,2},{7,3},{8,12},{9,13},{10,... | collective-permute-start | bytes 196616 | tf_op jit(solution)/shard_map/ppermute | solution.py:50
  16.9 5.1 %collective-permute-start.4 = (bf16[64,512]{1,0:T(8,128)(2,1)S(1)}, bf16[64,512]{1,0:T(8,128)(2,1)S(1)}, u32[]{:S(2)}, u32[]{:S(2)}) collective-permute-start(bf16[64,512]{1,0:T(8,128)(2,1)S(1)} %bitcast.17), channel_id=1, source_target_pairs={{0,2},{1,3},{2,0},{3,1},{4,6},{5,7},{6,4},{7,5},{8,10},{9,11},{10,... | collective-permute-start | bytes 196616 | tf_op jit(solution)/shard_map/ppermute | solution.py:50
  17.0 8.8 %collective-permute-start.3 = (bf16[64,512]{1,0:T(8,128)(2,1)S(1)}, bf16[64,512]{1,0:T(8,128)(2,1)S(1)}, u32[]{:S(2)}, u32[]{:S(2)}) collective-permute-start(bf16[64,512]{1,0:T(8,128)(2,1)S(1)} %bitcast.16), channel_id=1, source_target_pairs={{0,6},{1,7},{2,4},{3,5},{4,2},{5,3},{6,0},{7,1},{8,14},{9,15},{10,... | collective-permute-start | bytes 196616 | tf_op jit(solution)/shard_map/ppermute | solution.py:50
  19.8 6.0 %collective-permute-start.2 = (bf16[64,512]{1,0:T(8,128)(2,1)S(1)}, bf16[64,512]{1,0:T(8,128)(2,1)S(1)}, u32[]{:S(2)}, u32[]{:S(2)}) collective-permute-start(bf16[64,512]{1,0:T(8,128)(2,1)S(1)} %bitcast.15), channel_id=1, source_target_pairs={{0,4},{1,5},{2,6},{3,7},{4,0},{5,1},{6,2},{7,3},{8,12},{9,13},{10,... | collective-permute-start | bytes 196616 | tf_op jit(solution)/shard_map/ppermute | solution.py:50
  20.4 5.4 %collective-permute-start.1 = (bf16[64,512]{1,0:T(8,128)(2,1)S(1)}, bf16[64,512]{1,0:T(8,128)(2,1)S(1)}, u32[]{:S(2)}, u32[]{:S(2)}) collective-permute-start(bf16[64,512]{1,0:T(8,128)(2,1)S(1)} %bitcast.14), channel_id=1, source_target_pairs={{0,2},{1,3},{2,0},{3,1},{4,6},{5,7},{6,4},{7,5},{8,10},{9,11},{10,... | collective-permute-start | bytes 196616 | tf_op jit(solution)/shard_map/ppermute | solution.py:50
  22.1 5.3 %collective-permute-start.7 = (bf16[32,512]{1,0:T(8,128)(2,1)S(1)}, bf16[32,512]{1,0:T(8,128)(2,1)S(1)}, u32[]{:S(2)}, u32[]{:S(2)}) collective-permute-start(bf16[32,512]{1,0:T(8,128)(2,1)S(1)} %get-tuple-element.20), channel_id=1, source_target_pairs={{0,16},{1,17},{2,18},{3,19},{4,20},{5,21},{6,22},{7,23},{8,24},{9,... | collective-permute-start | bytes 98312 | tf_op jit(solution)/shard_map/ppermute | solution.py:50
  24.4 5.8 %collective-permute-start.8 = (bf16[32,512]{1,0:T(8,128)(2,1)S(1)}, bf16[32,512]{1,0:T(8,128)(2,1)S(1)}, u32[]{:S(2)}, u32[]{:S(2)}) collective-permute-start(bf16[32,512]{1,0:T(8,128)(2,1)S(1)} %get-tuple-element.21), channel_id=1, source_target_pairs={{0,24},{1,25},{2,26},{3,27},{4,28},{5,29},{6,30},{7,31},{8,16},{9,... | collective-permute-start | bytes 98312 | tf_op jit(solution)/shard_map/ppermute | solution.py:50
  25.9 4.3 %collective-permute-start.9 = (bf16[32,512]{1,0:T(8,128)(2,1)S(1)}, bf16[32,512]{1,0:T(8,128)(2,1)S(1)}, u32[]{:S(2)}, u32[]{:S(2)}) collective-permute-start(bf16[32,512]{1,0:T(8,128)(2,1)S(1)} %slice.73), channel_id=1, source_target_pairs={{0,8},{1,9},{2,10},{3,11},{4,12},{5,13},{6,14},{7,15},{8,0},{9,1},... | collective-permute-start | bytes 98312 | tf_op jit(solution)/shard_map/ppermute | solution.py:50

commit v5 on v4

--- a/solution.py
+++ b/solution.py
@@ -82,12 +82,12 @@
     copies[0].wait()
     source = tok[...].reshape(total, width) * jnp.asarray(0.5, bf16)
 
-    def activate(u, cols):
+    def activate(u, rows, cols):
         th = jnp.tanh(u)
         up = 1.0 + th
         act = u * up
-        hid[:, cols] = act.astype(bf16)
-        slope[:, cols] = up + act * (1.0 - th)
+        hid[rows, cols] = act.astype(bf16)
+        slope[rows, cols] = up + act * (1.0 - th)
 
     waiting = ()
     for part, (lo, hi) in enumerate(zip(bounds, bounds[1:])):
@@ -100,10 +100,11 @@
                 cot[s] = (cot[s].astype(f32) * live).astype(bf16)
         for first in range(lo, hi, tile):
             cols = pl.ds(first, tile)
-            u = dot(source, win[:, cols])
-            if waiting:
-                activate(*waiting)
-            waiting = (u, cols)
+            for top in range(0, total, lmax):
+                u = dot(source[top : top + lmax], win[:, cols])
+                if waiting:
+                    activate(*waiting)
+                waiting = (u, pl.ds(top, lmax), cols)
     dgated[...] = dot_nt(cot[...].reshape(total, width), wout[...])
     activate(*waiting)
 

time: 31.3 us -> 31 us (level)
  transfers between devices with their start and end apart: 10 -> 10, of which waited for: 5 -> 4; matrix products, arithmetic and copies ran while one was open for 0% -> 0% of each run, Pallas kernels for 0% -> 0%
where the time goes in v5:
time: 31 us; the launch traced here: 30.9 us
  starting transfers between devices  13.2 us (43%)
  Pallas kernels  9.27 us (30%)
  waiting for transfers between devices  6.48 us (21%)
  other arithmetic  1.13 us (4%)
  between operations  0.73 us (2%)
    ppermute x10, starting transfers between devices, send(): return lax.ppermute(x, AXES, perm)  13.2 us
    pallas_call x1, Pallas kernels, local_rows(): pl.pallas_call(functools.partial(local_kernel, wide, narrow, rows_dev), o...  9.27 us
    ppermute x10, waiting for transfers between devices, send(): return lax.ppermute(x, AXES, perm)  6.48 us
    sub x1, other arithmetic, adam_rows(): table - step_size * first_moment / scaled  0.77 us
  transfers between devices with their start and end apart: 10, of which 4 were waited for; matrix products, arithmetic and copies ran while one was open for 0% of the time, Pallas kernels for 0%

profile of v5, /device:TPU:0, one launch (start us, length us, event | category | flops | bytes accessed | tf_op | source)
XLA Modules:
  0.0 30.9 jit_solution(5724776816198236052)
XLA Ops:
  0.6 9.3 %local_rows.1 = (bf16[512,512]{1,0:T(8,128)(2,1)S(1)}, bf16[512,512]{1,0:T(8,128)(2,1)S(1)}) custom-call(s32[2]{0:T(128)} %len_hbm.1, s32[2,256]{1,0:T(2,128)} %rows_hbm.1, bf16[2,256,512]{2,1,0:T(8,128)(2,1)} %tok_hbm.1, bf16[2,256,512]{2,1,0:T(8,128)(2,1)} %cot_hbm.1, bf16[512,2048]{1,0:T(8,128)(2,1)} %win_hbm.1, bf16[512,512]{1,0:T(8,128)(2,1)} %wout_hbm.1), custom_call_target="tpu_custom_call" | custom-call | flops 2952790016 | bytes 4718592 | tf_op jit(solution)/shard_map/local_rows/pallas_call | solution.py:271
  9.9 0.0 copy-start
  9.9 0.0 copy-start.1
  9.9 0.0 copy-start.2
  9.9 0.6 %collective-permute-start = (bf16[512,512]{1,0:T(8,128)(2,1)S(1)}, bf16[512,512]{1,0:T(8,128)(2,1)S(1)}, u32[]{:S(2)}, u32[]{:S(2)}) collective-permute-start(bf16[512,512]{1,0:T(8,128)(2,1)S(1)} %get-tuple-element.6), channel_id=1, source_target_pairs={{0,1},{1,0},{2,3},{3,2},{4,5},{5,4},{6,7},{7,6},{8,9},{9,8},{10,11... | collective-permute-start | bytes 1572872 | tf_op jit(solution)/shard_map/ppermute | solution.py:50
  10.5 1.5 %collective-permute-done = bf16[512,512]{1,0:T(8,128)(2,1)S(1)} collective-permute-done((bf16[512,512]{1,0:T(8,128)(2,1)S(1)}, bf16[512,512]{1,0:T(8,128)(2,1)S(1)}, u32[]{:S(2)}, u32[]{:S(2)}) %collective-permute-start) | collective-permute-done | bytes 524320 | tf_op jit(solution)/shard_map/ppermute | solution.py:50
  12.0 0.1 add_convert_fusion
  12.2 3.9 %collective-permute-start.6 = (bf16[64,512]{1,0:T(8,128)(2,1)S(1)}, bf16[64,512]{1,0:T(8,128)(2,1)S(1)}, u32[]{:S(2)}, u32[]{:S(2)}) collective-permute-start(bf16[64,512]{1,0:T(8,128)(2,1)S(1)} %bitcast.19), channel_id=1, source_target_pairs={{0,6},{1,7},{2,4},{3,5},{4,2},{5,3},{6,0},{7,1},{8,14},{9,15},{10,... | collective-permute-start | bytes 196616 | tf_op jit(solution)/shard_map/ppermute | solution.py:50
  16.1 0.5 %collective-permute-start.5 = (bf16[64,512]{1,0:T(8,128)(2,1)S(1)}, bf16[64,512]{1,0:T(8,128)(2,1)S(1)}, u32[]{:S(2)}, u32[]{:S(2)}) collective-permute-start(bf16[64,512]{1,0:T(8,128)(2,1)S(1)} %bitcast.18), channel_id=1, source_target_pairs={{0,4},{1,5},{2,6},{3,7},{4,0},{5,1},{6,2},{7,3},{8,12},{9,13},{10,... | collective-permute-start | bytes 196616 | tf_op jit(solution)/shard_map/ppermute | solution.py:50
  16.6 0.1 collective-permute-start.4
  16.7 2.8 %collective-permute-start.3 = (bf16[64,512]{1,0:T(8,128)(2,1)S(1)}, bf16[64,512]{1,0:T(8,128)(2,1)S(1)}, u32[]{:S(2)}, u32[]{:S(2)}) collective-permute-start(bf16[64,512]{1,0:T(8,128)(2,1)S(1)} %bitcast.16), channel_id=1, source_target_pairs={{0,6},{1,7},{2,4},{3,5},{4,2},{5,3},{6,0},{7,1},{8,14},{9,15},{10,... | collective-permute-start | bytes 196616 | tf_op jit(solution)/shard_map/ppermute | solution.py:50
  19.6 0.5 %collective-permute-start.2 = (bf16[64,512]{1,0:T(8,128)(2,1)S(1)}, bf16[64,512]{1,0:T(8,128)(2,1)S(1)}, u32[]{:S(2)}, u32[]{:S(2)}) collective-permute-start(bf16[64,512]{1,0:T(8,128)(2,1)S(1)} %bitcast.15), channel_id=1, source_target_pairs={{0,4},{1,5},{2,6},{3,7},{4,0},{5,1},{6,2},{7,3},{8,12},{9,13},{10,... | collective-permute-start | bytes 196616 | tf_op jit(solution)/shard_map/ppermute | solution.py:50
  20.1 0.0 collective-permute-done.6
  20.1 0.5 %collective-permute-start.1 = (bf16[64,512]{1,0:T(8,128)(2,1)S(1)}, bf16[64,512]{1,0:T(8,128)(2,1)S(1)}, u32[]{:S(2)}, u32[]{:S(2)}) collective-permute-start(bf16[64,512]{1,0:T(8,128)(2,1)S(1)} %bitcast.14), channel_id=1, source_target_pairs={{0,2},{1,3},{2,0},{3,1},{4,6},{5,7},{6,4},{7,5},{8,10},{9,11},{10,... | collective-permute-start | bytes 196616 | tf_op jit(solution)/shard_map/ppermute | solution.py:50
  20.7 0.0 collective-permute-done.5
  20.7 1.0 %collective-permute-done.4 = bf16[64,512]{1,0:T(8,128)(2,1)S(1)} collective-permute-done((bf16[64,512]{1,0:T(8,128)(2,1)S(1)}, bf16[64,512]{1,0:T(8,128)(2,1)S(1)}, u32[]{:S(2)}, u32[]{:S(2)}) %collective-permute-start.4) | collective-permute-done | bytes 65568 | tf_op jit(solution)/shard_map/ppermute | solution.py:50
  21.8 2.4 %collective-permute-start.7 = (bf16[32,512]{1,0:T(8,128)(2,1)S(1)}, bf16[32,512]{1,0:T(8,128)(2,1)S(1)}, u32[]{:S(2)}, u32[]{:S(2)}) collective-permute-start(bf16[32,512]{1,0:T(8,128)(2,1)S(1)} %get-tuple-element.20), channel_id=1, source_target_pairs={{0,16},{1,17},{2,18},{3,19},{4,20},{5,21},{6,22},{7,23},{8,24},{9,... | collective-permute-start | bytes 98312 | tf_op jit(solution)/shard_map/ppermute | solution.py:50
  24.2 1.3 %collective-permute-start.8 = (bf16[32,512]{1,0:T(8,128)(2,1)S(1)}, bf16[32,512]{1,0:T(8,128)(2,1)S(1)}, u32[]{:S(2)}, u32[]{:S(2)}) collective-permute-start(bf16[32,512]{1,0:T(8,128)(2,1)S(1)} %get-tuple-element.21), channel_id=1, source_target_pairs={{0,24},{1,25},{2,26},{3,27},{4,28},{5,29},{6,30},{7,31},{8,16},{9,... | collective-permute-start | bytes 98312 | tf_op jit(solution)/shard_map/ppermute | solution.py:50
  25.5 0.0 collective-permute-done.3
  25.5 0.0 collective-permute-done.2
  25.5 0.0 collective-permute-done.1
  25.6 0.5 %collective-permute-start.9 = (bf16[32,512]{1,0:T(8,128)(2,1)S(1)}, bf16[32,512]{1,0:T(8,128)(2,1)S(1)}, u32[]{:S(2)}, u32[]{:S(2)}) collective-permute-start(bf16[32,512]{1,0:T(8,128)(2,1)S(1)} %slice.73), channel_id=1, source_target_pairs={{0,8},{1,9},{2,10},{3,11},{4,12},{5,13},{6,14},{7,15},{8,0},{9,1},... | collective-permute-start | bytes 98312 | tf_op jit(solution)/shard_map/ppermute | solution.py:50
  26.1 1.0 %collective-permute-done.7 = bf16[32,512]{1,0:T(8,128)(2,1)S(1)} collective-permute-done((bf16[32,512]{1,0:T(8,128)(2,1)S(1)}, bf16[32,512]{1,0:T(8,128)(2,1)S(1)}, u32[]{:S(2)}, u32[]{:S(2)}) %collective-permute-start.7) | collective-permute-done | bytes 32800 | tf_op jit(solution)/shard_map/ppermute | solution.py:50
  27.1 2.8 %collective-permute-done.8 = bf16[32,512]{1,0:T(8,128)(2,1)S(1)} collective-permute-done((bf16[32,512]{1,0:T(8,128)(2,1)S(1)}, bf16[32,512]{1,0:T(8,128)(2,1)S(1)}, u32[]{:S(2)}, u32[]{:S(2)}) %collective-permute-start.8) | collective-permute-done | bytes 32800 | tf_op jit(solution)/shard_map/ppermute | solution.py:50
  29.9 0.0 collective-permute-done.9
  29.9 0.1 multiply_reduce_fusion
  30.1 0.0 copy-done
  30.1 0.0 copy-done.1
  30.1 0.0 copy-done.2
  30.1 0.8 %divide_subtract_fusion = (f32[32,512]{1,0:T(8,128)}, f32[32,512]{1,0:T(8,128)}, f32[32,512]{1,0:T(8,128)}) fusion(f32[32,512]{1,0:T(8,128)S(1)} %copy-done, f32[32,512]{1,0:T(8,128)S(1)} %get-tuple-element.11, f32[32]{0:T(128)S(1)} %maximum_divide_fusion, f32[32,512]{1,0:T(8,128)S(1)} %copy-done.1, f32[32,512]{1,0:T(8,128)S(1)} %copy-done.2), kind=kLoop, calls=%fused_computation.14 | loop fusion | flops 212992 | bytes 458880 | tf_op jit(solution)/shard_map/sub | solution.py:311
  (6 shorter events, 0.1 us)
Async XLA Ops:
  9.9 20.2 %copy-start = (f32[32,512]{1,0:T(8,128)S(1)}, f32[32,512]{1,0:T(8,128)}, u32[]{:S(2)}) copy-start(f32[32,512]{1,0:T(8,128)} %param.15) | copy-start | bytes 196612
  9.9 20.2 %copy-start.1 = (f32[32,512]{1,0:T(8,128)S(1)}, f32[32,512]{1,0:T(8,128)}, u32[]{:S(2)}) copy-start(f32[32,512]{1,0:T(8,128)} %param.16) | copy-start | bytes 196612
  9.9 20.2 %copy-start.2 = (f32[32,512]{1,0:T(8,128)S(1)}, f32[32,512]{1,0:T(8,128)}, u32[]{:S(2)}) copy-start(f32[32,512]{1,0:T(8,128)} %param.17) | copy-start | bytes 196612
  9.9 2.1 %collective-permute-start = (bf16[512,512]{1,0:T(8,128)(2,1)S(1)}, bf16[512,512]{1,0:T(8,128)(2,1)S(1)}, u32[]{:S(2)}, u32[]{:S(2)}) collective-permute-start(bf16[512,512]{1,0:T(8,128)(2,1)S(1)} %get-tuple-element.6), channel_id=1, source_target_pairs={{0,1},{1,0},{2,3},{3,2},{4,5},{5,4},{6,7},{7,6},{8,9},{9,8},{10,11... | collective-permute-start | bytes 1572872 | tf_op jit(solution)/shard_map/ppermute | solution.py:50
  12.2 7.9 %collective-permute-start.6 = (bf16[64,512]{1,0:T(8,128)(2,1)S(1)}, bf16[64,512]{1,0:T(8,128)(2,1)S(1)}, u32[]{:S(2)}, u32[]{:S(2)}) collective-permute-start(bf16[64,512]{1,0:T(8,128)(2,1)S(1)} %bitcast.19), channel_id=1, source_target_pairs={{0,6},{1,7},{2,4},{3,5},{4,2},{5,3},{6,0},{7,1},{8,14},{9,15},{10,... | collective-permute-start | bytes 196616 | tf_op jit(solution)/shard_map/ppermute | solution.py:50
  16.1 4.6 %collective-permute-start.5 = (bf16[64,512]{1,0:T(8,128)(2,1)S(1)}, bf16[64,512]{1,0:T(8,128)(2,1)S(1)}, u32[]{:S(2)}, u32[]{:S(2)}) collective-permute-start(bf16[64,512]{1,0:T(8,128)(2,1)S(1)} %bitcast.18), channel_id=1, source_target_pairs={{0,4},{1,5},{2,6},{3,7},{4,0},{5,1},{6,2},{7,3},{8,12},{9,13},{10,... | collective-permute-start | bytes 196616 | tf_op jit(solution)/shard_map/ppermute | solution.py:50
  16.6 5.1 %collective-permute-start.4 = (bf16[64,512]{1,0:T(8,128)(2,1)S(1)}, bf16[64,512]{1,0:T(8,128)(2,1)S(1)}, u32[]{:S(2)}, u32[]{:S(2)}) collective-permute-start(bf16[64,512]{1,0:T(8,128)(2,1)S(1)} %bitcast.17), channel_id=1, source_target_pairs={{0,2},{1,3},{2,0},{3,1},{4,6},{5,7},{6,4},{7,5},{8,10},{9,11},{10,... | collective-permute-start | bytes 196616 | tf_op jit(solution)/shard_map/ppermute | solution.py:50
  16.7 8.8 %collective-permute-start.3 = (bf16[64,512]{1,0:T(8,128)(2,1)S(1)}, bf16[64,512]{1,0:T(8,128)(2,1)S(1)}, u32[]{:S(2)}, u32[]{:S(2)}) collective-permute-start(bf16[64,512]{1,0:T(8,128)(2,1)S(1)} %bitcast.16), channel_id=1, source_target_pairs={{0,6},{1,7},{2,4},{3,5},{4,2},{5,3},{6,0},{7,1},{8,14},{9,15},{10,... | collective-permute-start | bytes 196616 | tf_op jit(solution)/shard_map/ppermute | solution.py:50
  19.6 6.0 %collective-permute-start.2 = (bf16[64,512]{1,0:T(8,128)(2,1)S(1)}, bf16[64,512]{1,0:T(8,128)(2,1)S(1)}, u32[]{:S(2)}, u32[]{:S(2)}) collective-permute-start(bf16[64,512]{1,0:T(8,128)(2,1)S(1)} %bitcast.15), channel_id=1, source_target_pairs={{0,4},{1,5},{2,6},{3,7},{4,0},{5,1},{6,2},{7,3},{8,12},{9,13},{10,... | collective-permute-start | bytes 196616 | tf_op jit(solution)/shard_map/ppermute | solution.py:50
  20.1 5.4 %collective-permute-start.1 = (bf16[64,512]{1,0:T(8,128)(2,1)S(1)}, bf16[64,512]{1,0:T(8,128)(2,1)S(1)}, u32[]{:S(2)}, u32[]{:S(2)}) collective-permute-start(bf16[64,512]{1,0:T(8,128)(2,1)S(1)} %bitcast.14), channel_id=1, source_target_pairs={{0,2},{1,3},{2,0},{3,1},{4,6},{5,7},{6,4},{7,5},{8,10},{9,11},{10,... | collective-permute-start | bytes 196616 | tf_op jit(solution)/shard_map/ppermute | solution.py:50
  21.8 5.3 %collective-permute-start.7 = (bf16[32,512]{1,0:T(8,128)(2,1)S(1)}, bf16[32,512]{1,0:T(8,128)(2,1)S(1)}, u32[]{:S(2)}, u32[]{:S(2)}) collective-permute-start(bf16[32,512]{1,0:T(8,128)(2,1)S(1)} %get-tuple-element.20), channel_id=1, source_target_pairs={{0,16},{1,17},{2,18},{3,19},{4,20},{5,21},{6,22},{7,23},{8,24},{9,... | collective-permute-start | bytes 98312 | tf_op jit(solution)/shard_map/ppermute | solution.py:50
  24.2 5.7 %collective-permute-start.8 = (bf16[32,512]{1,0:T(8,128)(2,1)S(1)}, bf16[32,512]{1,0:T(8,128)(2,1)S(1)}, u32[]{:S(2)}, u32[]{:S(2)}) collective-permute-start(bf16[32,512]{1,0:T(8,128)(2,1)S(1)} %get-tuple-element.21), channel_id=1, source_target_pairs={{0,24},{1,25},{2,26},{3,27},{4,28},{5,29},{6,30},{7,31},{8,16},{9,... | collective-permute-start | bytes 98312 | tf_op jit(solution)/shard_map/ppermute | solution.py:50
  25.6 4.3 %collective-permute-start.9 = (bf16[32,512]{1,0:T(8,128)(2,1)S(1)}, bf16[32,512]{1,0:T(8,128)(2,1)S(1)}, u32[]{:S(2)}, u32[]{:S(2)}) collective-permute-start(bf16[32,512]{1,0:T(8,128)(2,1)S(1)} %slice.73), channel_id=1, source_target_pairs={{0,8},{1,9},{2,10},{3,11},{4,12},{5,13},{6,14},{7,15},{8,0},{9,1},... | collective-permute-start | bytes 98312 | tf_op jit(solution)/shard_map/ppermute | solution.py:50
